TPU v7x, 32 devices: a whole 2x2x4 slice. The times are simulated.
32 devices in a mesh: wide: 4 (over x, core), narrow: 8 (over z, y).
Axes of the slice: x: 2, y: 2, z: 4, core: 2. Of those that a mesh axis runs over, the one named last changes fastest.
Arguments:
- resid_in: bfloat16 [4096, 4096], P('wide', 'narrow'), may hold values from -6 to 6
- low_feat: bfloat16 [4096, 4096], P('wide', 'narrow'), may hold values from -6 to 6
- mid_feat: bfloat16 [4096, 4096], P('wide', 'narrow'), may hold values from -6 to 6
- segment: int32 [4096], P('wide'), may hold values from 0 to 31, never falling along the last dimension, each value on 1 to 256 neighbouring positions
- assign: int32 [4, 4], replicated, may hold values from 0 to 3, each once within a row
- attn_gain: float32 [4096], replicated, may hold values from 0.25 to 1.75
- qk_gain: float32 [2, 128], replicated, may hold values from 0.5 to 9
- query_weight: bfloat16 [4096, 4096], P(None, 'narrow'), may hold values from -0.09375 to 0.09375
- kv_weight: bfloat16 [4096, 512], P(None, 'narrow'), may hold values from -0.09375 to 0.09375
- out_weight: bfloat16 [4096, 4096], P('narrow'), may hold values from -0.09375 to 0.09375
- joining_weight: float32 [12288, 4096], P('wide', 'narrow'), may hold values from -0.0546875 to 0.0546875
- momentum: float32 [12288, 4096], P('wide', 'narrow'), may hold values from -0.06 to 0.06
Outputs:
- draft_error: float32 [4096, 4096], P('wide', 'narrow')
- new_joining: float32 [12288, 4096], P('wide', 'narrow')
- new_momentum: float32 [12288, 4096], P('wide', 'narrow')
Inputs may be any that keep to these rules, and one draw needn't show every extreme that they name: Each row of assign names every draft group exactly once. `segment`: ids never fall along the tokens.
All inputs are finite; a program needn't handle non-finite values.
Results may differ from a plain program's by a relative error of at most 0.004.
The roundings to bfloat16 on the way count: a program that leaves them out, or rounds other values in their place, can miss the bound.
Values may be sent and summed in bfloat16 or wider, within the bound.
No kernel may reach another device: no remote copies, remote signals or barrier semaphores. Data moves between devices by JAX's collectives and lax.ppermute only.
A program may use at most 192 MiB of HBM per device.

v0:
```python
import jax
import jax.numpy as jnp
from jax import lax
from jax.sharding import PartitionSpec as P

HEADS = 32
KVH = 2
HD = 128


mom_decay = 0.9
step_size = 0.5


def rms_scale(values, gain):
    return values * lax.rsqrt(jnp.mean(values * values, axis=-1, keepdims=True) + 1e-06) * gain


def on_device(
    resid_in,
    low_feat,
    mid_feat,
    segment,
    assign,
    attn_gain,
    qk_gain,
    query_weight,
    kv_weight,
    out_weight,
    joining_weight,
    momentum,
):
    groups = lax.axis_size("wide")
    tokens_local = resid_in.shape[0]
    block = tokens_local // groups
    heads_here = query_weight.shape[1] // HD
    per_head = HEADS // KVH
    width_kv = KVH * HD
    hidden_full = lax.all_gather(resid_in, "narrow", axis=1, tiled=True)
    normed = rms_scale(hidden_full.astype(jnp.float32), attn_gain).astype(jnp.bfloat16)
    queries = jnp.dot(normed, query_weight, preferred_element_type=jnp.float32).reshape(
        tokens_local, heads_here, HD
    )
    queries = rms_scale(queries, qk_gain[0]).astype(jnp.bfloat16)
    kv_part = jnp.dot(normed, kv_weight, preferred_element_type=jnp.float32).astype(jnp.bfloat16)
    keyvals = lax.all_gather(kv_part, "narrow", axis=1, tiled=True)
    kv_head = lax.axis_index("narrow") * heads_here // per_head
    keys = lax.dynamic_slice_in_dim(keyvals, kv_head * HD, HD, 1).astype(jnp.float32)
    keys = rms_scale(keys, qk_gain[1]).astype(jnp.bfloat16)
    value_head = lax.dynamic_slice_in_dim(keyvals, width_kv + kv_head * HD, HD, 1)
    scores = jnp.einsum("qhd,kd->hqk", queries, keys, preferred_element_type=jnp.float32) * HD ** (
        -0.5
    )
    positions = jnp.arange(tokens_local)
    allowed = (positions[:, None] >= positions[None, :]) & (segment[:, None] == segment[None, :])
    scores = jnp.where(allowed[None], scores, jnp.float32(-1e30))
    highest = jnp.max(scores, axis=-1, keepdims=True)
    expd = jnp.exp(scores - highest)
    probs = (expd / jnp.sum(expd, axis=-1, keepdims=True)).astype(jnp.bfloat16)
    context = jnp.einsum("hqk,kd->qhd", probs, value_head, preferred_element_type=jnp.float32)
    context = context.astype(jnp.bfloat16).reshape(tokens_local, heads_here * HD)
    out_cols = lax.all_to_all(out_weight, "narrow", split_axis=1, concat_axis=0, tiled=True)
    attn_cols = jnp.dot(
        lax.all_gather(context, "narrow", axis=1, tiled=True),
        out_cols,
        preferred_element_type=jnp.float32,
    )
    high = resid_in.astype(jnp.float32) + attn_cols
    valid = jnp.concatenate(
        [(segment[1:] == segment[:-1]).astype(jnp.float32), jnp.zeros((1,), jnp.float32)]
    )
    shifted = (
        jnp.concatenate([high[1:], jnp.zeros((1, high.shape[1]), jnp.float32)], axis=0)
        * valid[:, None]
    ).astype(jnp.bfloat16)
    stacked = jnp.stack([low_feat, mid_feat, high.astype(jnp.bfloat16)], axis=1)
    own_row = assign[lax.axis_index("wide")]
    slots = jnp.arange(groups, dtype=jnp.int32)
    inverse = jnp.sum(jnp.where(own_row[None, :] == slots[:, None], slots[None, :], 0), axis=1)
    send_feats = jnp.take(stacked.reshape(groups, block, 3, stacked.shape[2]), inverse, axis=0)
    send_target = jnp.take(shifted.reshape(groups, block, shifted.shape[1]), inverse, axis=0)
    send_valid = jnp.take(valid.astype(jnp.bfloat16).reshape(groups, block), inverse, axis=0)
    recv_feats, recv_target, recv_valid = (
        lax.all_to_all(send_feats, "wide", split_axis=0, concat_axis=0, tiled=True),
        lax.all_to_all(send_target, "wide", split_axis=0, concat_axis=0, tiled=True),
        lax.all_to_all(send_valid, "wide", split_axis=0, concat_axis=0, tiled=True),
    )
    gathered = lax.all_gather(recv_feats, "narrow", axis=3, tiled=True)
    inputs = gathered.reshape(tokens_local, -1)
    columns = inputs
    pred = jnp.dot(
        columns,
        lax.all_gather(joining_weight.astype(jnp.bfloat16), "wide", axis=0, tiled=True),
        preferred_element_type=jnp.float32,
    )
    target = recv_target.reshape(tokens_local, -1).astype(jnp.float32)
    mask_rows = recv_valid.reshape(tokens_local).astype(jnp.float32)
    error = (pred - target) * mask_rows[:, None]
    error_bf = error.astype(jnp.bfloat16)
    total_tokens = tokens_local * groups
    columns = inputs
    grads = lax.psum_scatter(
        lax.dot_general(
            columns, error_bf, (((0,), (0,)), ((), ())), preferred_element_type=jnp.float32
        )
        / total_tokens,
        "wide",
        scatter_dimension=0,
        tiled=True,
    )
    new_momentum = mom_decay * momentum + grads
    new_joining = joining_weight - step_size * new_momentum
    return (error, new_joining, new_momentum)


def solution(mesh):
    placed = (
        P("wide", "narrow"),
        P("wide", "narrow"),
        P("wide", "narrow"),
        P("wide"),
        P(),
        P(),
        P(),
        P(None, "narrow"),
        P(None, "narrow"),
        P("narrow", None),
        P("wide", "narrow"),
        P("wide", "narrow"),
    )
    return jax.shard_map(
        on_device,
        mesh=mesh,
        in_specs=placed,
        out_specs=(P("wide", "narrow"), P("wide", "narrow"), P("wide", "narrow")),
        check_vma=False,
    )
```

profile of v0, /device:TPU:0, one launch (start us, length us, event | category | flops | bytes accessed | tf_op | source)
XLA Modules:
  0.0 1279.0 jit_solution(16309112361379287032)
XLA Ops:
  7.2 0.7 all-gather.6.cloned.1.call-update
  8.0 2.3 fusion.9
  10.3 127.4 %all-gather.6.cloned.1.call-done = bf16[1024,4096]{1,0:T(8,128)(2,1)} async-done(((bf16[1024,512]{1,0:T(8,128)(2,1)}), bf16[1024,4096]{1,0:T(8,128)(2,1)}) %all-gather.6.cloned.1.call-update) | async-done | bytes 8388624 | tf_op jit(solution)/shard_map/all_gather | solution.py:39
  137.7 5.2 fusion.1
  143.0 0.5 copy-done.2
  143.5 3.5 fusion.18
  147.0 0.2 all-gather.10.cloned.1.call-start
  147.3 10.6 multiply_reduce_fusion
  157.9 1.9 copy.36
  159.8 25.8 %all-gather.8.cloned.1.call-done = bf16[1024,512]{0,1:T(8,128)(2,1)} async-done(((bf16[1024,64]{0,1:T(8,128)(2,1)}), bf16[1024,512]{0,1:T(8,128)(2,1)}) %all-gather.8.cloned.1.call-update) | async-done | bytes 1048592 | tf_op jit(solution)/shard_map/all_gather | solution.py:46
  185.6 1.0 fusion.22
  186.7 11.3 fusion.43
  197.9 8.1 fusion.17
  206.1 6.4 copy.39
  212.5 4.7 all-to-all-start
  217.2 0.3 all-gather.12.cloned.1.call-start
  217.5 0.7 fusion.39
  218.2 0.1 select_reduce_fusion
  218.3 179.6 %all-to-all-done = bf16[512,8,512]{0,2,1:T(8,128)(2,1)} async-done(((bf16[512,8,512]{0,2,1:T(8,128)(2,1)}), bf16[512,8,512]{0,2,1:T(8,128)(2,1)}, u32[]{:S(2)}, u32[]{:S(2)}) %all-to-all-start) | async-done | bytes 4194336 | tf_op jit(solution)/shard_map/all_to_all | solution.py:62
  397.9 6.4 copy.40
  404.3 5.8 all-gather.10.cloned.1.call-done
  410.1 9.5 fusion.48
  419.7 2.0 pad_maximum_fusion
  421.7 4.3 gather_fusion
  426.0 2.3 broadcast_select_fusion
  428.3 40.3 %all_to_all.35 = bf16[4,256,3,512]{3,1,2,0:T(8,128)(2,1)} all-to-all(bf16[4,256,3,512]{3,1,2,0:T(8,128)(2,1)S(1)} %broadcast_select_fusion), channel_id=1, replica_groups=mesh['wide'=4,'narrow'=8] {'wide'}, dimensions={0} | all-to-all | bytes 6291456 | tf_op jit(solution)/shard_map/all_to_all | solution.py:84
  468.7 4.9 convert_element_type.77
  473.6 0.1 fusion.33
  473.7 0.6 gather_fusion.2
  474.3 0.1 bitcast_select_fusion.4
  474.4 0.5 broadcast.151
  474.9 0.7 reduce
  475.5 0.6 reshape.187
  476.1 3.2 all-to-all-start.3
  479.4 0.2 slice.26
  479.6 0.2 multiply_convert_fusion
  479.8 0.6 gather_fusion.1
  480.4 1.1 broadcast_select_fusion.1
  481.6 1.4 all-to-all-done.3
  483.0 3.5 all-to-all-start.2
  486.6 459.5 %all-gather.12.cloned.1.call-done = bf16[4,256,3,4096]{3,1,2,0:T(8,128)(2,1)} async-done(((bf16[4,256,3,512]{3,1,2,0:T(8,128)(2,1)}), bf16[4,256,3,4096]{3,1,2,0:T(8,128)(2,1)}) %all-gather.12.cloned.1.call-update) | async-done | bytes 25165840 | tf_op jit(solution)/shard_map/all_gather | solution.py:88
  946.1 39.5 %copy.42 = bf16[4,256,3,4096]{1,0,3,2:T(4,128)(2,1)} copy(bf16[4,256,3,4096]{3,1,2,0:T(8,128)(2,1)} %all-gather.12.cloned.1.call-done) | data formatting | bytes 50331648 | tf_op jit(solution)/shard_map/all_gather | solution.py:88
  985.6 24.8 %copy.47 = bf16[1536,8,4,256]{3,1,2,0:T(8,128)(2,1)} copy(bf16[1536,8,4,256]{3,2,1,0:T(4,128)(2,1)} %bitcast.65) | data formatting | bytes 50331648
  1010.4 19.7 %all-gather.14.cloned.1.call-done = bf16[12288,512]{1,0:T(8,128)(2,1)} async-done(((bf16[3072,512]{1,0:T(8,128)(2,1)}), bf16[12288,512]{1,0:T(8,128)(2,1)}) %all-gather.14.cloned.1.call-update) | async-done | bytes 12582928 | tf_op jit(solution)/shard_map/all_gather | solution.py:93
  1030.2 22.5 %fusion.14 = f32[1024,512]{1,0:T(8,128)} fusion(bf16[1024,512]{1,0:T(8,128)(2,1)S(1)} %bitcast.73, bf16[1024,12288]{0,1:T(8,128)(2,1)} %bitcast.66, bf16[12288,512]{1,0:T(8,128)(2,1)} %all-gather.14.cloned.1.call-done, f32[1024]{0:T(1024)S(1)} %bitcast.77), kind=kOutput, calls=%fused_computation.27 | convolution fusion | flops 12886474752 | bytes 40898560 | tf_op jit(solution)/shard_map/dot_general | solution.py:91
  1052.7 23.3 %convolution_multiply_fusion = f32[12288,512]{1,0:T(8,128)} fusion(bf16[1024,12288]{0,1:T(8,128)(2,1)} %bitcast.67, f32[1024,512]{1,0:T(8,128)} %fusion.14), kind=kOutput, calls=%fused_computation.6 | convolution fusion | flops 12891717632 | bytes 52428800 | tf_op jit(solution)/shard_map/dot_general | solution.py:103
  1076.0 182.1 %reduce-scatter.2.cloned.1.call-done = f32[3072,512]{1,0:T(8,128)} async-done(((f32[12288,512]{1,0:T(8,128)}), f32[3072,512]{1,0:T(8,128)}) %reduce-scatter.2.cloned.1.call-update) | async-done | bytes 6291472 | tf_op jit(solution)/shard_map/reduce_scatter | solution.py:102
  1258.1 13.6 %multiply_subtract_fusion = (f32[3072,512]{1,0:T(8,128)}, f32[3072,512]{1,0:T(8,128)}) fusion(f32[3072,512]{1,0:T(8,128)} %param.22, f32[3072,512]{1,0:T(8,128)} %reduce-scatter.2.cloned.1.call-done, f32[3072,512]{1,0:T(8,128)} %param.23), kind=kLoop, calls=%fused_computation.18 | loop fusion | flops 6291456 | bytes 31457280 | tf_op jit(solution)/shard_map/sub | solution.py:112
  (36 shorter events, 0.4 us)
Async XLA Ops:
  7.2 135.8 %copy-start = (bf16[4096,64]{0,1:T(8,128)(2,1)S(1)}, bf16[4096,64]{0,1:T(8,128)(2,1)}, u32[]{:S(2)}) copy-start(bf16[4096,64]{0,1:T(8,128)(2,1)} %param.20) | copy-start | bytes 1572868
  7.2 135.8 %copy-start.7 = (f32[4096]{0:T(1024)S(1)}, f32[4096]{0:T(1024)}, u32[]{:S(2)}) copy-start(f32[4096]{0:T(1024)} %param.17) | copy-start | bytes 49156
  7.2 130.5 %all-gather.6.cloned.1.call-start = ((), (), s32[]{:S(2)}) async-start(), calls=%async_computation.5 | async-start | bytes 9437184 | tf_op jit(solution)/shard_map/all_gather | solution.py:39
  7.9 177.7 %all-gather.8.cloned.1.call-start = ((), (), s32[]{:S(2)}) async-start(), calls=%async_computation.6 | async-start | bytes 1179648 | tf_op jit(solution)/shard_map/all_gather | solution.py:46
  137.7 5.8 copy-start.2
  143.5 3.8 copy-start.6
  147.0 263.1 %all-gather.10.cloned.1.call-start = ((), (), s32[]{:S(2)}) async-start(), calls=%async_computation.7 | async-start | bytes 9437184 | tf_op jit(solution)/shard_map/all_gather | solution.py:64
  212.5 185.4 %all-to-all-start = ((bf16[512,8,512]{0,2,1:T(8,128)(2,1)}), bf16[512,8,512]{0,2,1:T(8,128)(2,1)}, u32[]{:S(2)}, u32[]{:S(2)}) async-start(bf16[512,8,512]{0,2,1:T(8,128)(2,1)} %bitcast.68), calls=%async_computation | async-start | bytes 8388608 | tf_op jit(solution)/shard_map/all_to_all | solution.py:62
  217.2 728.9 %all-gather.12.cloned.1.call-start = ((), (), s32[]{:S(2)}) async-start(), calls=%async_computation.8 | async-start | bytes 28311552 | tf_op jit(solution)/shard_map/all_gather | solution.py:88
  410.1 9.5 copy-start.3
  410.1 9.6 copy-start.4
  468.6 4.9 copy-start.5
  468.6 561.6 %all-gather.14.cloned.1.call-start = ((), (), s32[]{:S(2)}) async-start(), calls=%async_computation.9 | async-start | bytes 15728640 | tf_op jit(solution)/shard_map/all_gather | solution.py:93
  476.1 6.9 all-to-all-start.3
  483.0 547.2 %all-to-all-start.2 = ((bf16[4,256,512]{2,1,0:T(8,128)(2,1)}), bf16[4,256,512]{2,1,0:T(8,128)(2,1)S(1)}, u32[]{:S(2)}, u32[]{:S(2)}) async-start(bf16[4,256,512]{2,1,0:T(8,128)(2,1)} %broadcast_select_fusion.1), calls=%async_computation.2 | async-start | bytes 2097152 | tf_op jit(solution)/shard_map/all_to_all | solution.py:85
  486.6 771.5 %reduce-scatter.2.cloned.1.call-start = ((), (), s32[]{:S(2)}) async-start(), calls=%async_computation.10 | async-start | bytes 31457280 | tf_op jit(solution)/shard_map/reduce_scatter | solution.py:102
  1258.1 13.6 %copy-start.1 = (bf16[4096,64]{0,1:T(8,128)(2,1)S(1)}, bf16[4096,64]{0,1:T(8,128)(2,1)}, u32[]{:S(2)}) copy-start(bf16[4096,64]{0,1:T(8,128)(2,1)} %param.20) | copy-start | bytes 1572868
Sparse Core Ops, SparseCore 0:
  10.0 127.6 all-gather.5
  147.2 38.4 all-gather.7
  206.2 203.8 all-gather.9
  468.7 477.3 all-gather.11
  948.1 82.0 all-gather.13
  1076.2 181.8 reduce-scatter.1
where the time goes:
time: 1280 us
  waiting for transfers between devices  1000 us (78%)
  matrix products  88.8 us (7%)
  local copies, waits for them, and re-layouts  87.2 us (7%)
  blocking collectives  40.3 us (3%)
  other arithmetic  33.7 us (3%)
  between operations  14.8 us (1%)
    all_gather x1, waiting for transfers between devices, on_device(): gathered = lax.all_gather(recv_feats, 'narrow', axis=3, tiled=True)  459 us
    reduce_scatter x1, waiting for transfers between devices, on_device(): lax.psum_scatter(lax.dot_general(columns, error_bf, (((0,), (0,)), ((), (...  182 us
    all_to_all x1, waiting for transfers between devices, on_device(): lax.all_to_all(out_weight, 'narrow', split_axis=1, concat_axis=0, tiled=T...  180 us
    all_gather x1, waiting for transfers between devices, on_device(): hidden_full = lax.all_gather(resid_in, 'narrow', axis=1, tiled=True)  127 us
    all_to_all x1, blocking collectives, on_device(): lax.all_to_all(send_feats, 'wide', split_axis=0, concat_axis=0, tiled=True)  40.3 us
    all_gather x1, local copies, waits for them, and re-layouts, on_device(): gathered = lax.all_gather(recv_feats, 'narrow', axis=3, tiled=True)  39.5 us
    unnamed x20, local copies, waits for them, and re-layouts  32.4 us
    all_gather x1, waiting for transfers between devices, on_device(): keyvals = lax.all_gather(kv_part, 'narrow', axis=1, tiled=True)  25.8 us
  transfers between devices with their start and end apart: 9, of which 8 were waited for; matrix products, arithmetic and copies ran while one was open for 8% of the time, Pallas kernels for 0%

commit v1 on v0

v1 whole, which is shorter than its diff:
```python
import math

import jax
import jax.numpy as jnp
from jax import lax
from jax.experimental import pallas as pl
from jax.experimental.pallas import tpu as pltpu
from jax.sharding import PartitionSpec as P


KVH = 2
HD = 128
LONGEST = 256


mom_decay = 0.9
step_size = 0.5


def rms_scale(values, gain):
    return values * lax.rsqrt(jnp.mean(values * values, axis=-1, keepdims=True) + 1e-06) * gain


def ring_order(count):
    return list(range(0, count, 2)) + list(range(count - 1 - count % 2, 0, -2))


def ring_gather(shard, axis, base, extra, beside):
    count = lax.axis_size(axis)
    order = ring_order(count)
    place = [0] * count
    for at, member in enumerate(order):
        place[member] = at
    ahead = [(order[i], order[(i + 1) % count]) for i in range(count)]
    back = [(b, a) for a, b in ahead]
    own = lax.axis_index(axis)
    here = jnp.asarray(place, jnp.int32)[own]
    ring = jnp.asarray(order, jnp.int32)
    rows, width = shard.shape
    half = rows // 2
    parts = [shard[:half], shard[half:]]
    full = lax.dynamic_update_slice(base, shard, (0, own * width))
    moving = {(way, part): parts[part] for way in (0, 1) for part in (0, 1)}
    there = ring[(here + jnp.arange(count)) % count]
    for step in range(1, count // 2 + 1):
        last = count // 2 - step
        fresh = []
        for part in (0, 1):
            for way in (0, 1):
                if step == count // 2 and way != part:
                    continue
                got = lax.ppermute(moving[way, part], axis, back if way else ahead)
                source = ring[(here + step if way else here - step) % count]
                fresh.append((way, part, got, source))
        if last in beside:
            extra = beside[last](extra, full, there)
            extra, *held = lax.optimization_barrier((extra, *[item[2] for item in fresh]))
            fresh = [(way, part, got, source) for (way, part, _, source), got in zip(fresh, held)]
        for way, part, got, source in fresh:
            moving[way, part] = got
            full = lax.dynamic_update_slice(full, got, (part * half, source * width))
    return full, extra, there


def listed_gather(shard, axis):
    order = ring_order(lax.axis_size(axis))
    return lax.all_gather(shard, axis, axis=1, tiled=True, axis_index_groups=[order])


def wide_pieces(shard, axis):
    count = lax.axis_size(axis)
    pieces = [shard]
    for k in range(1, count):
        bit = k & -k
        pieces.append(lax.ppermute(pieces[k & (k - 1)], axis, [(i, i ^ bit) for i in range(count)]))
    return pieces


def head_pieces(part, axis):
    count = lax.axis_size(axis)
    share = count // KVH
    split = share // 2
    own = lax.axis_index(axis)

    def source(head, q):
        return head * split + q if q < split else KVH * split + head * split + q - split

    got = []
    for turn in range(share):
        perm = [
            (source(head, (j + turn) % share), head * share + j)
            for head in range(KVH)
            for j in range(share)
        ]
        got.append(lax.ppermute(part, axis, perm))
    stacked = jnp.stack(got + got)
    ordered = lax.dynamic_slice_in_dim(stacked, (share - own % share) % share, share, 0)
    rows = part.shape[0]
    key = jnp.swapaxes(ordered[:split], 0, 1).reshape(rows, HD)
    value = jnp.swapaxes(ordered[split:], 0, 1).reshape(rows, HD)
    return key, value


def project(hidden, order, gain, query_weight, kv_weight, head_gains):
    tokens, features = hidden.shape
    cols = query_weight.shape[1]
    width = features // len(order)
    rows = math.gcd(tokens, 256)

    def body(hidden_ref, gain_ref, query_ref, kv_ref, head_ref, q_ref, k_ref, v_ref):
        total = jnp.zeros((rows, 1), jnp.float32)
        for at in range(len(order)):
            values = hidden_ref[:, at * width : (at + 1) * width].astype(jnp.float32)
            total = total + jnp.sum(values * values, axis=-1, keepdims=True)
        scale = lax.rsqrt(total / features + 1e-06)
        product = jnp.zeros((rows, cols), jnp.float32)
        keyval = jnp.zeros((rows, 2 * HD), jnp.float32)
        for at, member in enumerate(order):
            values = hidden_ref[:, at * width : (at + 1) * width].astype(jnp.float32)
            picked = slice(member * width, (member + 1) * width)
            normed = (values * scale * gain_ref[:, picked]).astype(jnp.bfloat16)
            product = product + jnp.dot(
                normed, query_ref[picked, :], preferred_element_type=jnp.float32
            )
            keyval = keyval + jnp.dot(
                normed, kv_ref[picked, :], preferred_element_type=jnp.float32
            )
        for head in range(cols // HD):
            lanes = slice(head * HD, (head + 1) * HD)
            q_ref[:, lanes] = rms_scale(product[:, lanes], head_ref[0:1, :]).astype(jnp.bfloat16)
        keyval = keyval.astype(jnp.bfloat16)
        v_ref[...] = keyval[:, HD:]
        key = keyval[:, :HD].astype(jnp.float32)
        k_ref[...] = rms_scale(key, head_ref[1:2, :]).astype(jnp.bfloat16)

    whole = lambda i: (0, 0)
    row = lambda i: (i, 0)
    return pl.pallas_call(
        body,
        grid=(tokens // rows,),
        in_specs=[
            pl.BlockSpec((rows, features), row),
            pl.BlockSpec((1, features), whole),
            pl.BlockSpec((features, cols), whole),
            pl.BlockSpec((features, 2 * HD), whole),
            pl.BlockSpec((2, HD), whole),
        ],
        out_specs=[
            pl.BlockSpec((rows, cols), row),
            pl.BlockSpec((rows, HD), row),
            pl.BlockSpec((rows, HD), row),
        ],
        out_shape=[
            jax.ShapeDtypeStruct((tokens, cols), jnp.bfloat16),
            jax.ShapeDtypeStruct((tokens, HD), jnp.bfloat16),
            jax.ShapeDtypeStruct((tokens, HD), jnp.bfloat16),
        ],
        cost_estimate=pl.CostEstimate(
            flops=2 * tokens * features * (cols + 2 * HD),
            transcendentals=0,
            bytes_accessed=2 * tokens * features,
        ),
        name="project",
    )(hidden, gain.reshape(1, features), query_weight, kv_weight, head_gains)


def attend(queries, key, value, segment):
    tokens, cols = queries.shape
    rows = math.gcd(tokens, LONGEST) if tokens % LONGEST else LONGEST
    assert rows == LONGEST

    def body(q_ref, k0_ref, k1_ref, v0_ref, v1_ref, col_ref, row0_ref, row1_ref, out_ref):
        at = pl.program_id(0)
        kept = []
        for back, (k_ref, row_ref) in ((1, (k0_ref, row0_ref)), (0, (k1_ref, row1_ref))):
            keys = k_ref[...]
            ours = lax.broadcasted_iota(jnp.int32, (rows, rows), 0)
            theirs = lax.broadcasted_iota(jnp.int32, (rows, rows), 1) - back * rows
            allowed = (ours >= theirs) & (theirs + at * rows >= 0) & (col_ref[...] == row_ref[...])
            kept.append((keys, allowed))
        for head in range(cols // HD):
            lanes = slice(head * HD, (head + 1) * HD)
            query = q_ref[:, lanes]
            scores = []
            for keys, allowed in kept:
                score = lax.dot_general(
                    query, keys, (((1,), (1,)), ((), ())), preferred_element_type=jnp.float32
                )
                scores.append(jnp.where(allowed, score * HD ** (-0.5), jnp.float32(-1e30)))
            highest = jnp.maximum(
                jnp.max(scores[0], axis=-1, keepdims=True),
                jnp.max(scores[1], axis=-1, keepdims=True),
            )
            expd = [jnp.exp(score - highest) for score in scores]
            norm = jnp.sum(expd[0], axis=-1, keepdims=True) + jnp.sum(
                expd[1], axis=-1, keepdims=True
            )
            probs = [(e / norm).astype(jnp.bfloat16) for e in expd]
            context = jnp.dot(
                probs[0], v0_ref[...], preferred_element_type=jnp.float32
            ) + jnp.dot(probs[1], v1_ref[...], preferred_element_type=jnp.float32)
            out_ref[:, lanes] = context.astype(jnp.bfloat16)

    before = lambda i: (jnp.maximum(i - 1, 0), 0)
    current = lambda i: (i, 0)
    before_row = lambda i: (0, jnp.maximum(i - 1, 0))
    current_row = lambda i: (0, i)
    return pl.pallas_call(
        body,
        grid=(tokens // rows,),
        in_specs=[
            pl.BlockSpec((rows, cols), current),
            pl.BlockSpec((rows, HD), before),
            pl.BlockSpec((rows, HD), current),
            pl.BlockSpec((rows, HD), before),
            pl.BlockSpec((rows, HD), current),
            pl.BlockSpec((rows, 1), current),
            pl.BlockSpec((1, rows), before_row),
            pl.BlockSpec((1, rows), current_row),
        ],
        out_specs=pl.BlockSpec((rows, cols), current),
        out_shape=jax.ShapeDtypeStruct((tokens, cols), jnp.bfloat16),
        cost_estimate=pl.CostEstimate(
            flops=32 * tokens * rows * cols, transcendentals=0, bytes_accessed=4 * tokens * cols
        ),
        name="attend",
    )(
        queries,
        key,
        key,
        value,
        value,
        segment.reshape(tokens, 1),
        segment.reshape(1, tokens),
        segment.reshape(1, tokens),
    )


def predict(feat, places, table, joined, first, base, target=None, valid=None):
    tokens = feat.shape[0]
    steps = table.shape[0]
    inner = feat.shape[1] // lax.axis_size("narrow")
    cols = joined.shape[1]
    ends = target is not None

    def body(places_ref, table_ref, *refs):
        at = pl.program_id(0)
        feat_ref, joined_ref = refs[:2]
        out_ref = refs[-2] if ends else refs[-1]
        product = jnp.dot(feat_ref[...], joined_ref[...], preferred_element_type=jnp.float32)

        @pl.when(at == 0)
        def _():
            out_ref[...] = product if base is None else refs[2][...] + product

        @pl.when(at > 0)
        def _():
            out_ref[...] += product

        if ends:

            @pl.when(at == steps - 1)
            def _():
                error = (out_ref[...] - refs[3][...].astype(jnp.float32)) * refs[4][...]
                out_ref[...] = error
                refs[-1][...] = error.astype(jnp.bfloat16)

    whole = lambda i, places_ref, table_ref: (0, 0)
    in_specs = [
        pl.BlockSpec((tokens, inner), lambda i, places_ref, table_ref: (0, places_ref[i])),
        pl.BlockSpec(
            (inner, cols), lambda i, places_ref, table_ref: (first // inner + table_ref[i], 0)
        ),
    ]
    operands = [feat, joined]
    if base is not None:
        in_specs.append(pl.BlockSpec((tokens, cols), whole))
        operands.append(base)
    out_specs = pl.BlockSpec((tokens, cols), whole)
    out_shape = jax.ShapeDtypeStruct((tokens, cols), jnp.float32)
    if ends:
        in_specs += [pl.BlockSpec((tokens, cols), whole), pl.BlockSpec((tokens, 1), whole)]
        operands += [target, valid.reshape(tokens, 1)]
        out_specs = [out_specs, pl.BlockSpec((tokens, cols), whole)]
        out_shape = [out_shape, jax.ShapeDtypeStruct((tokens, cols), jnp.bfloat16)]
    return pl.pallas_call(
        body,
        grid_spec=pltpu.PrefetchScalarGridSpec(
            num_scalar_prefetch=2, grid=(steps,), in_specs=in_specs, out_specs=out_specs
        ),
        out_shape=out_shape,
        cost_estimate=pl.CostEstimate(
            flops=2 * tokens * steps * inner * cols,
            transcendentals=0,
            bytes_accessed=2 * tokens * steps * inner,
        ),
        name="predict",
    )(places, table, *operands)


def grad_rows(first, pieces, width, tables, feats, errors, out_dtype):
    per = tables[0].shape[0]
    kinds = len(tables)
    tokens, cols = errors[0].shape

    def body(first_ref, table_ref, *refs):
        out_ref = refs[-1]
        error_refs = refs[-1 - len(errors) : -1]
        piece = first_ref[0] + pl.program_id(0)
        for at in range(kinds):

            @pl.when(piece // per == at)
            def _(at=at):
                total = None
                for group, error_ref in enumerate(error_refs):
                    term = lax.dot_general(
                        refs[group * kinds + at][...],
                        error_ref[...],
                        (((0,), (0,)), ((), ())),
                        preferred_element_type=jnp.float32,
                    )
                    total = term if total is None else total + term
                out_ref[...] = total.astype(out_dtype)

    def feat_map(at):
        def of(i, first_ref, table_ref):
            piece = jnp.clip(first_ref[0] + i - at * per, 0, per - 1)
            return (0, table_ref[at * per + piece])

        return of

    whole = lambda i, first_ref, table_ref: (0, 0)
    in_specs = [
        pl.BlockSpec((tokens, width), feat_map(at)) for _ in errors for at in range(kinds)
    ]
    in_specs += [pl.BlockSpec((tokens, cols), whole) for _ in errors]
    return pl.pallas_call(
        body,
        grid_spec=pltpu.PrefetchScalarGridSpec(
            num_scalar_prefetch=2,
            grid=(pieces,),
            in_specs=in_specs,
            out_specs=pl.BlockSpec((width, cols), lambda i, first_ref, table_ref: (i, 0)),
        ),
        out_shape=jax.ShapeDtypeStruct((pieces * width, cols), out_dtype),
        cost_estimate=pl.CostEstimate(
            flops=4 * tokens * pieces * width * cols,
            transcendentals=0,
            bytes_accessed=4 * tokens * pieces * width,
        ),
        name="grad_rows",
    )(first.reshape(1), jnp.concatenate(tables), *[f for group in feats for f in group], *errors)


def step_on_device(
    resid_in,
    low_feat,
    mid_feat,
    segment,
    assign,
    attn_gain,
    qk_gain,
    query_weight,
    kv_weight,
    out_weight,
    joining_weight,
    momentum,
):
    groups = lax.axis_size("wide")
    narrow = lax.axis_size("narrow")
    mine = lax.axis_index("wide").astype(jnp.int32)
    tokens_local = resid_in.shape[0]
    block = tokens_local // groups
    features = query_weight.shape[0]
    width = features // narrow
    order = ring_order(narrow)
    partner = [(i, i ^ 1) for i in range(groups)]

    hidden_full = listed_gather(resid_in, "narrow")
    low_full = listed_gather(low_feat, "narrow")
    mid_full = listed_gather(mid_feat, "narrow")

    share = out_weight.shape[0] // groups
    rows_mine = lax.dynamic_slice_in_dim(out_weight, mine * share, share, 0)
    got = lax.all_to_all(rows_mine, "narrow", split_axis=1, concat_axis=0, tiled=True)
    out_pieces = wide_pieces(got, "wide")
    rows_here = joining_weight.shape[0]
    joined_pieces = wide_pieces(joining_weight.astype(jnp.bfloat16), "wide")

    kv_share = features // groups
    kv_rows = lax.dynamic_slice_in_dim(kv_weight, mine * kv_share, kv_share, 0)
    kv_rows = jnp.concatenate(head_pieces(kv_rows, "narrow"), axis=1)
    kv_own = jnp.zeros((features, 2 * HD), kv_weight.dtype)
    for k, piece in enumerate(wide_pieces(kv_rows, "wide")):
        kv_own = lax.dynamic_update_slice(kv_own, piece, ((mine ^ k) * kv_share, 0))

    hidden_full, kv_own, joined_pieces, out_pieces = lax.optimization_barrier(
        (hidden_full, kv_own, joined_pieces, out_pieces)
    )
    out_cols = jnp.zeros((narrow, groups, share, width), out_weight.dtype)
    for k, piece in enumerate(out_pieces):
        out_cols = lax.dynamic_update_slice(
            out_cols, piece.reshape(narrow, 1, share, width), (0, mine ^ k, 0, 0)
        )
    out_cols = out_cols.reshape(narrow * groups * share, width)
    joined = jnp.zeros((rows_here * groups, joining_weight.shape[1]), jnp.bfloat16)
    for k, piece in enumerate(joined_pieces):
        joined = lax.dynamic_update_slice(joined, piece, ((mine ^ k) * rows_here, 0))

    queries, key, value = project(
        hidden_full, order, attn_gain, query_weight, kv_own, qk_gain
    )
    context = attend(queries, key, value, segment)

    listed = jnp.asarray(order, jnp.int32)
    natural = jnp.arange(narrow, dtype=jnp.int32)
    low_other = lax.ppermute(low_full, "wide", partner)
    mid_other = lax.ppermute(mid_full, "wide", partner)

    def of_low(pred, full, there):
        return predict(low_full, natural, listed, joined, 0, None)

    def of_mid(pred, full, there):
        return predict(mid_full, natural, listed, joined, features, pred)

    def of_high(pred, full, there):
        near = jnp.concatenate([there[: narrow // 2], there[narrow // 2 + 1 :]])
        return predict(full, near, near, joined, 2 * features, pred)

    context_full, pred, _ = ring_gather(context, "narrow", hidden_full, None, {1: of_low})
    attn_cols = jnp.dot(context_full, out_cols, preferred_element_type=jnp.float32)
    high = resid_in.astype(jnp.float32) + attn_cols
    valid = jnp.concatenate(
        [(segment[1:] == segment[:-1]).astype(jnp.float32), jnp.zeros((1,), jnp.float32)]
    )
    target = (
        jnp.concatenate([high[1:], jnp.zeros((1, high.shape[1]), jnp.float32)], axis=0)
        * valid[:, None]
    ).astype(jnp.bfloat16)
    high_full, pred, there = ring_gather(
        high.astype(jnp.bfloat16), "narrow", context_full, pred, {1: of_mid, 0: of_high}
    )
    last = there[narrow // 2 : narrow // 2 + 1]
    high_other = lax.ppermute(high_full, "wide", partner)

    error, error_bf = predict(
        high_full, last, last, joined, 2 * features, pred, target, valid
    )
    error_other = lax.ppermute(error_bf, "wide", partner)

    own_row = assign[mine]
    slots = jnp.arange(groups, dtype=jnp.int32)
    inverse = jnp.sum(jnp.where(own_row[None, :] == slots[:, None], slots[None, :], 0), axis=1)
    sent = []
    for k in sorted(range(groups), key=lambda k: -k):
        piece = lax.dynamic_slice_in_dim(error, inverse[mine ^ k] * block, block, 0)
        if k:
            piece = lax.ppermute(piece, "wide", [(i, i ^ k) for i in range(groups)])
        sent.append((k, piece))

    place = jnp.asarray([order.index(member) for member in range(narrow)], jnp.int32)
    tables = (place, place, natural)
    feats = ((low_full, mid_full, high_full), (low_other, mid_other, high_other))
    per_chunk = rows_here // width

    def rows_of(member, dtype):
        return grad_rows(
            member * per_chunk, per_chunk, width, tables, feats, (error_bf, error_other), dtype
        )

    far = []
    for bit in range(2, groups, 2):
        away = rows_of(mine ^ bit, jnp.bfloat16)
        far.append(lax.ppermute(away, "wide", [(i, i ^ bit) for i in range(groups)]))
    grads = rows_of(mine, jnp.float32)
    error_out = jnp.zeros_like(error)
    for k, piece in sent:
        error_out = lax.dynamic_update_slice(error_out, piece, ((mine ^ k) * block, 0))
    for piece in far:
        grads = grads + piece.astype(jnp.float32)
    grads = grads / (tokens_local * groups)
    new_momentum = mom_decay * momentum + grads
    new_joining = joining_weight - step_size * new_momentum
    return (error_out, new_joining, new_momentum)


def solution(mesh):
    placed = (
        P("wide", "narrow"),
        P("wide", "narrow"),
        P("wide", "narrow"),
        P("wide"),
        P(),
        P(),
        P(),
        P(None, "narrow"),
        P(None, "narrow"),
        P("narrow", None),
        P("wide", "narrow"),
        P("wide", "narrow"),
    )
    return jax.shard_map(
        step_on_device,
        mesh=mesh,
        in_specs=placed,
        out_specs=(P("wide", "narrow"), P("wide", "narrow"), P("wide", "narrow")),
        check_vma=False,
    )
```

time: 1280 us -> 640 us (0.50)
  waiting for transfers between devices: 1000 us -> 329 us
  Pallas kernels: 0 us -> 95.6 us
  matrix products: 88.8 us -> 8.23 us
  blocking collectives: 40.3 us -> 0 us
  starting transfers between devices: 12 us -> 51.4 us
  between operations: 14.8 us -> 36.1 us
    all_gather x5 -> x3, waiting for transfers between devices: 638 us -> 47.5 us  [listed_gather(): lax.all_gather(shard, axis, axis=1, tiled=True, axis_index_groups=[order])]
    ppermute x0 -> x49, waiting for transfers between devices: none -> 280 us  [the longest x28 109 us: ring_gather(): got = lax.ppermute(moving[way, part], axis, back if way else ahead)]
    reduce_scatter x1 -> x0, waiting for transfers between devices: 182 us -> none  [on_device(): lax.psum_scatter(lax.dot_general(columns, error_bf, (((0,), (0,)), ((), (...]
    all_to_all x3 -> x1, waiting for transfers between devices: 181 us -> 0.01 us  [step_on_device(): lax.all_to_all(rows_mine, 'narrow', split_axis=1, concat_axis=0, tiled=True)]
    pallas_call x0 -> x8, Pallas kernels: none -> 95.6 us  [the longest x4 43.7 us: predict(): pl.pallas_call(body, grid_spec=pltpu.PrefetchScalarGridSpec(num_scalar_pr...]
    dot_general x6 -> x1, matrix products: 77.6 us -> 8.23 us  [step_on_device(): jnp.dot(context_full, out_cols, preferred_element_type=jnp.float32)]
    dynamic_update_slice x0 -> x44, local copies, waits for them, and re-layouts: none -> 68.2 us  [the longest x28 36.1 us: ring_gather(): full = lax.dynamic_update_slice(full, got, (part * half, source * width))]
    ppermute x0 -> x49, starting transfers between devices: none -> 45.5 us  [the longest x28 28.6 us: ring_gather(): got = lax.ppermute(moving[way, part], axis, back if way else ahead)]
  transfers between devices with their start and end apart: 9 -> 53, of which waited for: 8 -> 23; matrix products, arithmetic and copies ran while one was open for 8% -> 17% of each run, Pallas kernels for 0% -> 13%
where the time goes in v1:
time: 640 us; the launch traced here: 638 us
  waiting for transfers between devices  329 us (51%)
  Pallas kernels  95.6 us (15%)
  local copies, waits for them, and re-layouts  95.4 us (15%)
  starting transfers between devices  51.4 us (8%)
  between operations  36.1 us (6%)
  other arithmetic  22.1 us (3%)
  matrix products  8.23 us (1%)
    ppermute x28, waiting for transfers between devices, ring_gather(): got = lax.ppermute(moving[way, part], axis, back if way else ahead)  109 us
    ppermute x3, waiting for transfers between devices, step_on_device(): piece = lax.ppermute(piece, 'wide', [(i, i ^ k) for i in range(groups)])  82.2 us
    ppermute x9, waiting for transfers between devices, wide_pieces(): lax.ppermute(pieces[k & k - 1], axis, [(i, i ^ bit) for i in range(count)])  49.5 us
    all_gather x3, waiting for transfers between devices, listed_gather(): lax.all_gather(shard, axis, axis=1, tiled=True, axis_index_groups=[order])  47.5 us
    pallas_call x4, Pallas kernels, predict(): pl.pallas_call(body, grid_spec=pltpu.PrefetchScalarGridSpec(num_scalar_pr...  43.7 us
    dynamic_update_slice x28, local copies, waits for them, and re-layouts, ring_gather(): full = lax.dynamic_update_slice(full, got, (part * half, source * width))  36.1 us
    ppermute x4, waiting for transfers between devices, head_pieces(): got.append(lax.ppermute(part, axis, perm))  34.2 us
    pallas_call x2, Pallas kernels, grad_rows(): pl.pallas_call(body, grid_spec=pltpu.PrefetchScalarGridSpec(num_scalar_pr...  28.9 us
  transfers between devices with their start and end apart: 53, of which 23 were waited for; matrix products, arithmetic and copies ran while one was open for 17% of the time, Pallas kernels for 13%

profile of v1, /device:TPU:0, one launch (start us, length us, event | category | flops | bytes accessed | tf_op | source)
XLA Modules:
  0.0 637.9 jit_solution(13718449484077752522)
XLA Ops:
  8.7 4.9 convert_element_type.16
  13.6 3.0 collective-permute-start.8
  19.2 5.8 all-to-all-start
  25.8 5.7 collective-permute-start.1
  32.6 33.1 %collective-permute-done.1 = bf16[1024,64]{0,1:T(8,128)(2,1)S(1)} collective-permute-done((bf16[1024,64]{0,1:T(8,128)(2,1)S(1)}, bf16[1024,64]{0,1:T(8,128)(2,1)S(1)}, u32[]{:S(2)}, u32[]{:S(2)}) %collective-permute-start.1) | collective-permute-done | bytes 131104 | tf_op jit(solution)/shard_map/ppermute | solution.py:95
  65.7 19.3 %collective-permute-done.8 = bf16[3072,512]{1,0:T(8,128)(2,1)} collective-permute-done((bf16[3072,512]{1,0:T(8,128)(2,1)}, bf16[3072,512]{1,0:T(8,128)(2,1)}, u32[]{:S(2)}, u32[]{:S(2)}) %collective-permute-start.8) | collective-permute-done | bytes 3145760 | tf_op jit(solution)/shard_map/ppermute | solution.py:75
  93.6 20.2 %collective-permute-done.11 = bf16[1024,512]{1,0:T(8,128)(2,1)S(1)} collective-permute-done((bf16[1024,512]{1,0:T(8,128)(2,1)S(1)}, bf16[1024,512]{1,0:T(8,128)(2,1)S(1)}, u32[]{:S(2)}, u32[]{:S(2)}) %collective-permute-start.11) | collective-permute-done | bytes 1048608 | tf_op jit(solution)/shard_map/ppermute | solution.py:75
  113.8 9.6 %collective-permute-done.5 = bf16[1024,256]{1,0:T(8,128)(2,1)S(1)} collective-permute-done((bf16[1024,256]{1,0:T(8,128)(2,1)S(1)}, bf16[1024,256]{1,0:T(8,128)(2,1)S(1)}, u32[]{:S(2)}, u32[]{:S(2)}) %collective-permute-start.5) | collective-permute-done | bytes 524320 | tf_op jit(solution)/shard_map/ppermute | solution.py:75
  143.5 13.8 %project.1 = (bf16[1024,512]{1,0:T(8,128)(2,1)}, bf16[1024,128]{1,0:T(8,128)(2,1)}, bf16[1024,128]{1,0:T(8,128)(2,1)}) custom-call(bf16[1024,4096]{1,0:T(8,128)(2,1)} %all-gather.4.cloned.1.call-done.hidden_ref, f32[1,4096]{1,0:T(1,128)} %bitcast.89, bf16[4096,512]{1,0:T(8,128)(2,1)} %query_ref.1, ...), custom_call_target="tpu_custom_call" | custom-call | flops 6442450944 | bytes 8388608 | tf_op jit(solution)/shard_map/project/pallas_call | solution.py:138
  157.3 9.3 %attend.1 = bf16[1024,512]{1,0:T(8,128)(2,1)} custom-call(bf16[1024,512]{1,0:T(8,128)(2,1)} %get-tuple-element.33.q_ref, bf16[1024,128]{1,0:T(8,128)(2,1)} %get-tuple-element.34.k0_ref.k1_ref, bf16[1024,128]{1,0:T(8,128)(2,1)} %get-tuple-element.34.k0_ref.k1_ref, bf16[1024,128]{1,0:T(8,128)(2,1)} %get-tuple-element.35.v0_ref.v1_ref, ...), custom_call_target="tpu_custom_call" | custom-call | flops 4294967296 | bytes 2097152 | tf_op jit(solution)/shard_map/attend/pallas_call | solution.py:208
  167.9 1.9 collective-permute-start.13
  172.0 2.4 constant_dynamic-update-slice_fusion.26
  174.3 2.5 broadcast_in_dim.34
  177.9 2.3 constant_dynamic-update-slice_fusion.13
  181.2 5.3 broadcast_in_dim.33
  186.4 3.8 constant_dynamic-update-slice_fusion.21
  190.2 3.8 constant_dynamic-update-slice_fusion.20
  194.0 3.8 constant_dynamic-update-slice_fusion.19
  197.8 2.3 constant_dynamic-update-slice_fusion.11
  200.1 3.9 constant_dynamic-update-slice_fusion.18.refs_1_
  206.0 10.4 %collective-permute-done.15 = bf16[512,512]{1,0:T(8,128)(2,1)S(1)} collective-permute-done((bf16[512,512]{1,0:T(8,128)(2,1)S(1)}, bf16[512,512]{1,0:T(8,128)(2,1)S(1)}, u32[]{:S(2)}, u32[]{:S(2)}) %collective-permute-start.15) | collective-permute-done | bytes 524320 | tf_op jit(solution)/shard_map/ppermute | solution.py:52
  218.5 47.5 %all-gather.6.cloned.1.call-done.refs_0_ = bf16[1024,4096]{1,0:T(8,128)(2,1)} async-done(((bf16[1024,512]{1,0:T(8,128)(2,1)}), bf16[1024,4096]{1,0:T(8,128)(2,1)}) %all-gather.6.cloned.1.call-update) | async-done | bytes 8388624 | tf_op jit(solution)/shard_map/all_gather | solution.py:67
  266.4 12.3 %predict.4.refs_2_ = f32[1024,512]{1,0:T(8,128)} custom-call(s32[8]{0:T(128)} %iota.19.places_ref, s32[8]{0:T(128)} %constant.222.clone.table_ref, bf16[1024,4096]{1,0:T(8,128)(2,1)} %all-gather.6.cloned.1.call-done.refs_0_, bf16[12288,512]{1,0:T(8,128)(2,1)} %constant_dynamic-update-slice_fusion.18.refs_1_), custom_call_target="tpu_custom_call" | custom-call | flops 4294967296 | bytes 8388608 | tf_op jit(solution)/shard_map/predict/pallas_call | solution.py:286
  278.8 2.0 constant_dynamic-update-slice_fusion.25
  280.8 1.9 constant_dynamic-update-slice_fusion.24
  292.2 16.6 %collective-permute-done.21 = bf16[512,512]{1,0:T(8,128)(2,1)S(1)} collective-permute-done((bf16[512,512]{1,0:T(8,128)(2,1)S(1)}, bf16[512,512]{1,0:T(8,128)(2,1)S(1)}, u32[]{:S(2)}, u32[]{:S(2)}) %collective-permute-start.21) | collective-permute-done | bytes 524320 | tf_op jit(solution)/shard_map/ppermute | solution.py:52
  310.1 20.7 %collective-permute-done.23 = bf16[512,512]{1,0:T(8,128)(2,1)S(1)} collective-permute-done((bf16[512,512]{1,0:T(8,128)(2,1)}, bf16[512,512]{1,0:T(8,128)(2,1)S(1)}, u32[]{:S(2)}, u32[]{:S(2)}) %collective-permute-start.23) | collective-permute-done | bytes 524320 | tf_op jit(solution)/shard_map/ppermute | solution.py:52
  338.5 18.9 %collective-permute-done.25 = bf16[512,512]{1,0:T(8,128)(2,1)S(1)} collective-permute-done((bf16[512,512]{1,0:T(8,128)(2,1)S(1)}, bf16[512,512]{1,0:T(8,128)(2,1)S(1)}, u32[]{:S(2)}, u32[]{:S(2)}) %collective-permute-start.25) | collective-permute-done | bytes 524320 | tf_op jit(solution)/shard_map/ppermute | solution.py:52
  360.6 8.2 %convert_add_fusion = f32[1024,512]{1,0:T(8,128)S(1)} fusion(bf16[1024,512]{1,0:T(8,128)(2,1)S(1)} %copy-done.7, bf16[1024,4096]{1,0:T(8,128)(2,1)} %constant_dynamic-update-slice_fusion.38, bf16[4096,512]{1,0:T(8,128)(2,1)} %bitcast.40), kind=kOutput, calls=%fused_computation.4 | convolution fusion | flops 4296015872 | bytes 15728640 | tf_op jit(solution)/shard_map/dot_general | solution.py:431
  382.3 15.2 %collective-permute-done.27 = bf16[512,512]{1,0:T(8,128)(2,1)} collective-permute-done((bf16[512,512]{1,0:T(8,128)(2,1)}, bf16[512,512]{1,0:T(8,128)(2,1)}, u32[]{:S(2)}, u32[]{:S(2)}) %collective-permute-start.27) | collective-permute-done | bytes 524320 | tf_op jit(solution)/shard_map/ppermute | solution.py:52
  399.5 11.8 %collective-permute-done.29 = bf16[512,512]{1,0:T(8,128)(2,1)} collective-permute-done((bf16[512,512]{1,0:T(8,128)(2,1)}, bf16[512,512]{1,0:T(8,128)(2,1)}, u32[]{:S(2)}, u32[]{:S(2)}) %collective-permute-start.29) | collective-permute-done | bytes 524320 | tf_op jit(solution)/shard_map/ppermute | solution.py:52
  413.9 13.1 %predict.5.refs_2_ = f32[1024,512]{1,0:T(8,128)} custom-call(s32[8]{0:T(128)} %iota.20.places_ref, s32[8]{0:T(128)} %constant.222.clone.table_ref, bf16[1024,4096]{1,0:T(8,128)(2,1)} %all-gather.8.cloned.1.call-done.refs_0_.refs_1_, bf16[12288,512]{1,0:T(8,128)(2,1)} %constant_dynamic-update-slice_fusion.18.refs_1_, f32[1024,512]{1,0:T(8,128)} %predict.4.refs_2_), custom_call_target="tpu_custom_call" | custom-call | flops 4294967296 | bytes 8388608 | tf_op jit(solution)/shard_map/predict/pallas_call | solution.py:286
  427.0 1.9 constant_dynamic-update-slice_fusion.9
  428.9 1.9 constant_dynamic-update-slice_fusion.8
  430.8 1.9 constant_dynamic-update-slice_fusion.37
  442.3 1.9 constant_dynamic-update-slice_fusion.34
  444.3 3.4 collective-permute-done.35
  448.1 7.6 %collective-permute-done.37 = bf16[512,512]{1,0:T(8,128)(2,1)S(1)} collective-permute-done((bf16[512,512]{1,0:T(8,128)(2,1)}, bf16[512,512]{1,0:T(8,128)(2,1)S(1)}, u32[]{:S(2)}, u32[]{:S(2)}) %collective-permute-start.37) | collective-permute-done | bytes 524320 | tf_op jit(solution)/shard_map/ppermute | solution.py:52
  458.0 2.0 constant_dynamic-update-slice_fusion.5
  461.7 2.0 constant_dynamic-update-slice_fusion.32.refs_0_
  463.6 12.1 %predict.6.refs_2_ = f32[1024,512]{1,0:T(8,128)} custom-call(s32[7]{0:T(128)} %pad_add_fusion.places_ref.table_ref, s32[7]{0:T(128)} %pad_add_fusion.places_ref.table_ref, bf16[1024,4096]{1,0:T(8,128)(2,1)} %constant_dynamic-update-slice_fusion.32.refs_0_, bf16[12288,512]{1,0:T(8,128)(2,1)} %constant_dynamic-update-slice_fusion.18.refs_1_, ...), custom_call_target="tpu_custom_call" | custom-call | flops 3758096384 | bytes 7340032 | tf_op jit(solution)/shard_map/predict/pallas_call | solution.py:286
  480.8 6.2 predict.7
  487.4 4.9 collective-permute-done.47.refs_7_
  493.3 14.1 %grad_rows.3 = bf16[3072,512]{1,0:T(8,128)(2,1)} custom-call(s32[1]{0:T(128)} %bitcast.56.first_ref, s32[24]{0:T(128)} %constant.226.table_ref, bf16[1024,4096]{1,0:T(8,128)(2,1)} %all-gather.6.cloned.1.call-done.refs_0_, bf16[1024,4096]{1,0:T(8,128)(2,1)} %all-gather.8.cloned.1.call-done.refs_0_.refs_1_, ...), custom_call_target="tpu_custom_call" | custom-call | flops 6442450944 | bytes 12582912 | tf_op jit(solution)/shard_map/grad_rows/pallas_call | solution.py:337
  516.5 72.4 %collective-permute-done.41 = f32[256,512]{1,0:T(8,128)} collective-permute-done((f32[256,512]{1,0:T(8,128)S(1)}, f32[256,512]{1,0:T(8,128)}, u32[]{:S(2)}, u32[]{:S(2)}) %collective-permute-start.41) | collective-permute-done | bytes 524320 | tf_op jit(solution)/shard_map/ppermute | solution.py:458
  590.3 9.8 %collective-permute-done.42 = f32[256,512]{1,0:T(8,128)} collective-permute-done((f32[256,512]{1,0:T(8,128)S(1)}, f32[256,512]{1,0:T(8,128)}, u32[]{:S(2)}, u32[]{:S(2)}) %collective-permute-start.42) | collective-permute-done | bytes 524320 | tf_op jit(solution)/shard_map/ppermute | solution.py:458
  603.4 14.8 %grad_rows.2 = f32[3072,512]{1,0:T(8,128)} custom-call(s32[1]{0:T(128)} %bitcast.55.first_ref, s32[24]{0:T(128)} %constant.226.table_ref, bf16[1024,4096]{1,0:T(8,128)(2,1)} %all-gather.6.cloned.1.call-done.refs_0_, bf16[1024,4096]{1,0:T(8,128)(2,1)} %all-gather.8.cloned.1.call-done.refs_0_.refs_1_, ...), custom_call_target="tpu_custom_call" | custom-call | flops 6442450944 | bytes 12582912 | tf_op jit(solution)/shard_map/grad_rows/pallas_call | solution.py:337
  618.2 13.2 %multiply_subtract_fusion = (f32[3072,512]{1,0:T(8,128)}, f32[3072,512]{1,0:T(8,128)}) fusion(f32[3072,512]{1,0:T(8,128)} %param.28, f32[3072,512]{1,0:T(8,128)} %grad_rows.2, bf16[3072,512]{1,0:T(8,128)(2,1)} %collective-permute-done.48, f32[3072,512]{1,0:T(8,128)} %param.29), kind=kLoop, calls=%fused_computation.1 | loop fusion | flops 11010048 | bytes 34603008 | tf_op jit(solution)/shard_map/sub | solution.py:483
  (183 shorter events, 96.7 us)
Async XLA Ops:
  7.2 136.4 %all-gather.4.cloned.1.call-start = ((), (), s32[]{:S(2)}) async-start(), calls=%async_computation.1 | async-start | bytes 9437184 | tf_op jit(solution)/shard_map/all_gather | solution.py:67
  7.9 258.0 %all-gather.6.cloned.1.call-start = ((), (), s32[]{:S(2)}) async-start(), calls=%async_computation.2 | async-start | bytes 9437184 | tf_op jit(solution)/shard_map/all_gather | solution.py:67
  8.7 404.7 %all-gather.8.cloned.1.call-start = ((), (), s32[]{:S(2)}) async-start(), calls=%async_computation.3 | async-start | bytes 9437184 | tf_op jit(solution)/shard_map/all_gather | solution.py:67
  13.6 71.4 %collective-permute-start.8 = (bf16[3072,512]{1,0:T(8,128)(2,1)}, bf16[3072,512]{1,0:T(8,128)(2,1)}, u32[]{:S(2)}, u32[]{:S(2)}) collective-permute-start(bf16[3072,512]{1,0:T(8,128)(2,1)} %convert_element_type.16), channel_id=1, source_target_pairs={{0,16},{8,24},{16,0},{24,8},{1,17},{9,25},{17,1},{25,9},{2,18},{10... | collective-permute-start | bytes 9437192 | tf_op jit(solution)/shard_map/ppermute | solution.py:75
  19.2 67.0 %all-to-all-start = ((bf16[128,8,512]{0,2,1:T(8,128)(2,1)}), bf16[128,8,512]{0,2,1:T(8,128)(2,1)S(1)}, u32[]{:S(2)}, u32[]{:S(2)}) async-start(bf16[128,8,512]{0,2,1:T(8,128)(2,1)} %bitcast.80), calls=%async_computation | async-start | bytes 2097152 | tf_op jit(solution)/shard_map/all_to_all | solution.py:385
  25.8 39.9 %collective-permute-start.1 = (bf16[1024,64]{0,1:T(8,128)(2,1)S(1)}, bf16[1024,64]{0,1:T(8,128)(2,1)S(1)}, u32[]{:S(2)}, u32[]{:S(2)}) collective-permute-start(bf16[1024,64]{0,1:T(8,128)(2,1)S(1)} %constant_dynamic-slice_fusion.7), channel_id=1, source_target_pairs={{1,0},{4,1},{5,2},{0,3},{3,4},{6,5},{7,6},{2,7},{9,8},{12,9},{13,1... | collective-permute-start | bytes 393224 | tf_op jit(solution)/shard_map/ppermute | solution.py:95
  31.4 53.5 %collective-permute-start.2 = (bf16[1024,64]{0,1:T(8,128)(2,1)S(1)}, bf16[1024,64]{0,1:T(8,128)(2,1)S(1)}, u32[]{:S(2)}, u32[]{:S(2)}) collective-permute-start(bf16[1024,64]{0,1:T(8,128)(2,1)S(1)} %constant_dynamic-slice_fusion.7), channel_id=1, source_target_pairs={{4,0},{5,1},{0,2},{1,3},{6,4},{7,5},{2,6},{3,7},{12,8},{13,9},{8,1... | collective-permute-start | bytes 393224 | tf_op jit(solution)/shard_map/ppermute | solution.py:95
  31.4 54.7 %collective-permute-start.3 = (bf16[1024,64]{0,1:T(8,128)(2,1)S(1)}, bf16[1024,64]{0,1:T(8,128)(2,1)S(1)}, u32[]{:S(2)}, u32[]{:S(2)}) collective-permute-start(bf16[1024,64]{0,1:T(8,128)(2,1)S(1)} %constant_dynamic-slice_fusion.7), channel_id=1, source_target_pairs={{5,0},{0,1},{1,2},{4,3},{7,4},{2,5},{3,6},{6,7},{13,8},{8,9},{9,10... | collective-permute-start | bytes 393224 | tf_op jit(solution)/shard_map/ppermute | solution.py:95
  32.5 110.9 %collective-permute-start.7 = (bf16[3072,512]{1,0:T(8,128)(2,1)}, bf16[3072,512]{1,0:T(8,128)(2,1)}, u32[]{:S(2)}, u32[]{:S(2)}) collective-permute-start(bf16[3072,512]{1,0:T(8,128)(2,1)} %convert_element_type.16), channel_id=1, source_target_pairs={{0,8},{8,0},{16,24},{24,16},{1,9},{9,1},{17,25},{25,17},{2,10},{10... | collective-permute-start | bytes 9437192 | tf_op jit(solution)/shard_map/ppermute | solution.py:75
  84.9 58.6 %collective-permute-start.9 = (bf16[3072,512]{1,0:T(8,128)(2,1)}, bf16[3072,512]{1,0:T(8,128)(2,1)}, u32[]{:S(2)}, u32[]{:S(2)}) collective-permute-start(bf16[3072,512]{1,0:T(8,128)(2,1)} %collective-permute-done.8), channel_id=1, source_target_pairs={{0,8},{8,0},{16,24},{24,16},{1,9},{9,1},{17,25},{25,17},{2,10},{10... | collective-permute-start | bytes 9437192 | tf_op jit(solution)/shard_map/ppermute | solution.py:75
  87.7 26.1 %collective-permute-start.11 = (bf16[1024,512]{1,0:T(8,128)(2,1)S(1)}, bf16[1024,512]{1,0:T(8,128)(2,1)S(1)}, u32[]{:S(2)}, u32[]{:S(2)}) collective-permute-start(bf16[1024,512]{1,0:T(8,128)(2,1)S(1)} %bitcast.76), channel_id=1, source_target_pairs={{0,16},{8,24},{16,0},{24,8},{1,17},{9,25},{17,1},{25,9},{2,18},{10... | collective-permute-start | bytes 3145736 | tf_op jit(solution)/shard_map/ppermute | solution.py:75
  91.7 31.7 %collective-permute-start.5 = (bf16[1024,256]{1,0:T(8,128)(2,1)S(1)}, bf16[1024,256]{1,0:T(8,128)(2,1)S(1)}, u32[]{:S(2)}, u32[]{:S(2)}) collective-permute-start(bf16[1024,256]{1,0:T(8,128)(2,1)S(1)} %get-tuple-element.72), channel_id=1, source_target_pairs={{0,16},{8,24},{16,0},{24,8},{1,17},{9,25},{17,1},{25,9},{2,18},{10... | collective-permute-start | bytes 1572872 | tf_op jit(solution)/shard_map/ppermute | solution.py:75
  93.4 50.1 %collective-permute-start.10 = (bf16[1024,512]{1,0:T(8,128)(2,1)S(1)}, bf16[1024,512]{1,0:T(8,128)(2,1)}, u32[]{:S(2)}, u32[]{:S(2)}) collective-permute-start(bf16[1024,512]{1,0:T(8,128)(2,1)S(1)} %bitcast.77), channel_id=1, source_target_pairs={{0,8},{8,0},{16,24},{24,16},{1,9},{9,1},{17,25},{25,17},{2,10},{10... | collective-permute-start | bytes 3145736 | tf_op jit(solution)/shard_map/ppermute | solution.py:75
  113.8 29.7 %collective-permute-start.12 = (bf16[1024,512]{1,0:T(8,128)(2,1)S(1)}, bf16[1024,512]{1,0:T(8,128)(2,1)}, u32[]{:S(2)}, u32[]{:S(2)}) collective-permute-start(bf16[1024,512]{1,0:T(8,128)(2,1)S(1)} %collective-permute-done.11), channel_id=1, source_target_pairs={{0,8},{8,0},{16,24},{24,16},{1,9},{9,1},{17,25},{25,17},{2,10},{10... | collective-permute-start | bytes 3145736 | tf_op jit(solution)/shard_map/ppermute | solution.py:75
  123.4 18.2 %collective-permute-start.6 = (bf16[1024,256]{1,0:T(8,128)(2,1)S(1)}, bf16[1024,256]{1,0:T(8,128)(2,1)}, u32[]{:S(2)}, u32[]{:S(2)}) collective-permute-start(bf16[1024,256]{1,0:T(8,128)(2,1)S(1)} %collective-permute-done.5), channel_id=1, source_target_pairs={{0,8},{8,0},{16,24},{24,16},{1,9},{9,1},{17,25},{25,17},{2,10},{10... | collective-permute-start | bytes 1572872 | tf_op jit(solution)/shard_map/ppermute | solution.py:75
  167.9 36.1 %collective-permute-start.13 = (bf16[512,512]{1,0:T(8,128)(2,1)S(1)}, bf16[512,512]{1,0:T(8,128)(2,1)}, u32[]{:S(2)}, u32[]{:S(2)}) collective-permute-start(bf16[512,512]{1,0:T(8,128)(2,1)S(1)} %get-tuple-element.69), channel_id=1, source_target_pairs={{0,2},{2,4},{4,6},{6,7},{7,5},{5,3},{3,1},{1,0},{8,10},{10,12},{12... | collective-permute-start | bytes 1572872 | tf_op jit(solution)/shard_map/ppermute | solution.py:52
  169.8 36.0 %collective-permute-start.14 = (bf16[512,512]{1,0:T(8,128)(2,1)S(1)}, bf16[512,512]{1,0:T(8,128)(2,1)}, u32[]{:S(2)}, u32[]{:S(2)}) collective-permute-start(bf16[512,512]{1,0:T(8,128)(2,1)S(1)} %get-tuple-element.69), channel_id=1, source_target_pairs={{2,0},{4,2},{6,4},{7,6},{5,7},{3,5},{1,3},{0,1},{10,8},{12,10},{14... | collective-permute-start | bytes 1572872 | tf_op jit(solution)/shard_map/ppermute | solution.py:52
  170.0 46.5 %collective-permute-start.15 = (bf16[512,512]{1,0:T(8,128)(2,1)S(1)}, bf16[512,512]{1,0:T(8,128)(2,1)S(1)}, u32[]{:S(2)}, u32[]{:S(2)}) collective-permute-start(bf16[512,512]{1,0:T(8,128)(2,1)S(1)} %get-tuple-element.68), channel_id=1, source_target_pairs={{0,2},{2,4},{4,6},{6,7},{7,5},{5,3},{3,1},{1,0},{8,10},{10,12},{12... | collective-permute-start | bytes 1572872 | tf_op jit(solution)/shard_map/ppermute | solution.py:52
  171.8 46.5 %collective-permute-start.16 = (bf16[512,512]{1,0:T(8,128)(2,1)S(1)}, bf16[512,512]{1,0:T(8,128)(2,1)S(1)}, u32[]{:S(2)}, u32[]{:S(2)}) collective-permute-start(bf16[512,512]{1,0:T(8,128)(2,1)S(1)} %get-tuple-element.68), channel_id=1, source_target_pairs={{2,0},{4,2},{6,4},{7,6},{5,7},{3,5},{1,3},{0,1},{10,8},{12,10},{14... | collective-permute-start | bytes 1572872 | tf_op jit(solution)/shard_map/ppermute | solution.py:52
  204.0 78.8 %collective-permute-start.17 = (bf16[512,512]{1,0:T(8,128)(2,1)}, bf16[512,512]{1,0:T(8,128)(2,1)S(1)}, u32[]{:S(2)}, u32[]{:S(2)}) collective-permute-start(bf16[512,512]{1,0:T(8,128)(2,1)} %collective-permute-done.13), channel_id=1, source_target_pairs={{0,2},{2,4},{4,6},{6,7},{7,5},{5,3},{3,1},{1,0},{8,10},{10,12},{12... | collective-permute-start | bytes 1572872 | tf_op jit(solution)/shard_map/ppermute | solution.py:52
  205.8 78.3 %collective-permute-start.18 = (bf16[512,512]{1,0:T(8,128)(2,1)}, bf16[512,512]{1,0:T(8,128)(2,1)S(1)}, u32[]{:S(2)}, u32[]{:S(2)}) collective-permute-start(bf16[512,512]{1,0:T(8,128)(2,1)} %collective-permute-done.14), channel_id=1, source_target_pairs={{2,0},{4,2},{6,4},{7,6},{5,7},{3,5},{1,3},{0,1},{10,8},{12,10},{14... | collective-permute-start | bytes 1572872 | tf_op jit(solution)/shard_map/ppermute | solution.py:52
  216.4 68.3 %collective-permute-start.19 = (bf16[512,512]{1,0:T(8,128)(2,1)S(1)}, bf16[512,512]{1,0:T(8,128)(2,1)}, u32[]{:S(2)}, u32[]{:S(2)}) collective-permute-start(bf16[512,512]{1,0:T(8,128)(2,1)S(1)} %collective-permute-done.15), channel_id=1, source_target_pairs={{0,2},{2,4},{4,6},{6,7},{7,5},{5,3},{3,1},{1,0},{8,10},{10,12},{12... | collective-permute-start | bytes 1572872 | tf_op jit(solution)/shard_map/ppermute | solution.py:52
  218.3 67.9 %collective-permute-start.20 = (bf16[512,512]{1,0:T(8,128)(2,1)S(1)}, bf16[512,512]{1,0:T(8,128)(2,1)S(1)}, u32[]{:S(2)}, u32[]{:S(2)}) collective-permute-start(bf16[512,512]{1,0:T(8,128)(2,1)S(1)} %collective-permute-done.16), channel_id=1, source_target_pairs={{2,0},{4,2},{6,4},{7,6},{5,7},{3,5},{1,3},{0,1},{10,8},{12,10},{14... | collective-permute-start | bytes 1572872 | tf_op jit(solution)/shard_map/ppermute | solution.py:52
  282.7 26.0 %collective-permute-start.21 = (bf16[512,512]{1,0:T(8,128)(2,1)S(1)}, bf16[512,512]{1,0:T(8,128)(2,1)S(1)}, u32[]{:S(2)}, u32[]{:S(2)}) collective-permute-start(bf16[512,512]{1,0:T(8,128)(2,1)S(1)} %collective-permute-done.17), channel_id=1, source_target_pairs={{0,2},{2,4},{4,6},{6,7},{7,5},{5,3},{3,1},{1,0},{8,10},{10,12},{12... | collective-permute-start | bytes 1572872 | tf_op jit(solution)/shard_map/ppermute | solution.py:52
  284.1 26.0 %collective-permute-start.22 = (bf16[512,512]{1,0:T(8,128)(2,1)S(1)}, bf16[512,512]{1,0:T(8,128)(2,1)S(1)}, u32[]{:S(2)}, u32[]{:S(2)}) collective-permute-start(bf16[512,512]{1,0:T(8,128)(2,1)S(1)} %collective-permute-done.18), channel_id=1, source_target_pairs={{2,0},{4,2},{6,4},{7,6},{5,7},{3,5},{1,3},{0,1},{10,8},{12,10},{14... | collective-permute-start | bytes 1572872 | tf_op jit(solution)/shard_map/ppermute | solution.py:52
  284.8 46.0 %collective-permute-start.23 = (bf16[512,512]{1,0:T(8,128)(2,1)}, bf16[512,512]{1,0:T(8,128)(2,1)S(1)}, u32[]{:S(2)}, u32[]{:S(2)}) collective-permute-start(bf16[512,512]{1,0:T(8,128)(2,1)} %collective-permute-done.19), channel_id=1, source_target_pairs={{0,2},{2,4},{4,6},{6,7},{7,5},{5,3},{3,1},{1,0},{8,10},{10,12},{12... | collective-permute-start | bytes 1572872 | tf_op jit(solution)/shard_map/ppermute | solution.py:52
  286.2 46.0 %collective-permute-start.24 = (bf16[512,512]{1,0:T(8,128)(2,1)S(1)}, bf16[512,512]{1,0:T(8,128)(2,1)S(1)}, u32[]{:S(2)}, u32[]{:S(2)}) collective-permute-start(bf16[512,512]{1,0:T(8,128)(2,1)S(1)} %collective-permute-done.20), channel_id=1, source_target_pairs={{2,0},{4,2},{6,4},{7,6},{5,7},{3,5},{1,3},{0,1},{10,8},{12,10},{14... | collective-permute-start | bytes 1572872 | tf_op jit(solution)/shard_map/ppermute | solution.py:52
  332.1 25.3 %collective-permute-start.25 = (bf16[512,512]{1,0:T(8,128)(2,1)S(1)}, bf16[512,512]{1,0:T(8,128)(2,1)S(1)}, u32[]{:S(2)}, u32[]{:S(2)}) collective-permute-start(bf16[512,512]{1,0:T(8,128)(2,1)S(1)} %collective-permute-done.21), channel_id=1, source_target_pairs={{0,2},{2,4},{4,6},{6,7},{7,5},{5,3},{3,1},{1,0},{8,10},{10,12},{12... | collective-permute-start | bytes 1572872 | tf_op jit(solution)/shard_map/ppermute | solution.py:52
  334.5 25.2 %collective-permute-start.26 = (bf16[512,512]{1,0:T(8,128)(2,1)S(1)}, bf16[512,512]{1,0:T(8,128)(2,1)S(1)}, u32[]{:S(2)}, u32[]{:S(2)}) collective-permute-start(bf16[512,512]{1,0:T(8,128)(2,1)S(1)} %collective-permute-done.24), channel_id=1, source_target_pairs={{2,0},{4,2},{6,4},{7,6},{5,7},{3,5},{1,3},{0,1},{10,8},{12,10},{14... | collective-permute-start | bytes 1572872 | tf_op jit(solution)/shard_map/ppermute | solution.py:52
  371.1 26.3 %collective-permute-start.27 = (bf16[512,512]{1,0:T(8,128)(2,1)}, bf16[512,512]{1,0:T(8,128)(2,1)}, u32[]{:S(2)}, u32[]{:S(2)}) collective-permute-start(bf16[512,512]{1,0:T(8,128)(2,1)} %get-tuple-element.67), channel_id=1, source_target_pairs={{0,2},{2,4},{4,6},{6,7},{7,5},{5,3},{3,1},{1,0},{8,10},{10,12},{12... | collective-permute-start | bytes 1572872 | tf_op jit(solution)/shard_map/ppermute | solution.py:52
  372.6 26.3 %collective-permute-start.28 = (bf16[512,512]{1,0:T(8,128)(2,1)}, bf16[512,512]{1,0:T(8,128)(2,1)}, u32[]{:S(2)}, u32[]{:S(2)}) collective-permute-start(bf16[512,512]{1,0:T(8,128)(2,1)} %get-tuple-element.67), channel_id=1, source_target_pairs={{2,0},{4,2},{6,4},{7,6},{5,7},{3,5},{1,3},{0,1},{10,8},{12,10},{14... | collective-permute-start | bytes 1572872 | tf_op jit(solution)/shard_map/ppermute | solution.py:52
  373.2 38.2 %collective-permute-start.29 = (bf16[512,512]{1,0:T(8,128)(2,1)}, bf16[512,512]{1,0:T(8,128)(2,1)}, u32[]{:S(2)}, u32[]{:S(2)}) collective-permute-start(bf16[512,512]{1,0:T(8,128)(2,1)} %get-tuple-element.66), channel_id=1, source_target_pairs={{0,2},{2,4},{4,6},{6,7},{7,5},{5,3},{3,1},{1,0},{8,10},{10,12},{12... | collective-permute-start | bytes 1572872 | tf_op jit(solution)/shard_map/ppermute | solution.py:52
  374.6 37.1 %collective-permute-start.30 = (bf16[512,512]{1,0:T(8,128)(2,1)}, bf16[512,512]{1,0:T(8,128)(2,1)S(1)}, u32[]{:S(2)}, u32[]{:S(2)}) collective-permute-start(bf16[512,512]{1,0:T(8,128)(2,1)} %get-tuple-element.66), channel_id=1, source_target_pairs={{2,0},{4,2},{6,4},{7,6},{5,7},{3,5},{1,3},{0,1},{10,8},{12,10},{14... | collective-permute-start | bytes 1572872 | tf_op jit(solution)/shard_map/ppermute | solution.py:52
  382.3 110.1 %collective-permute-start.44 = (bf16[1024,4096]{1,0:T(8,128)(2,1)}, bf16[1024,4096]{1,0:T(8,128)(2,1)}, u32[]{:S(2)}, u32[]{:S(2)}) collective-permute-start(bf16[1024,4096]{1,0:T(8,128)(2,1)} %all-gather.6.cloned.1.call-done.refs_0_), channel_id=1, source_target_pairs={{0,8},{8,0},{16,24},{24,16},{1,9},{9,1},{17,25},{25,17},{2,10},{10... | collective-permute-start | bytes 25165832 | tf_op jit(solution)/shard_map/ppermute | solution.py:417
  397.5 35.3 %collective-permute-start.31 = (bf16[512,512]{1,0:T(8,128)(2,1)}, bf16[512,512]{1,0:T(8,128)(2,1)S(1)}, u32[]{:S(2)}, u32[]{:S(2)}) collective-permute-start(bf16[512,512]{1,0:T(8,128)(2,1)} %collective-permute-done.27), channel_id=1, source_target_pairs={{0,2},{2,4},{4,6},{6,7},{7,5},{5,3},{3,1},{1,0},{8,10},{10,12},{12... | collective-permute-start | bytes 1572872 | tf_op jit(solution)/shard_map/ppermute | solution.py:52
  398.9 34.2 %collective-permute-start.32 = (bf16[512,512]{1,0:T(8,128)(2,1)}, bf16[512,512]{1,0:T(8,128)(2,1)}, u32[]{:S(2)}, u32[]{:S(2)}) collective-permute-start(bf16[512,512]{1,0:T(8,128)(2,1)} %collective-permute-done.28), channel_id=1, source_target_pairs={{2,0},{4,2},{6,4},{7,6},{5,7},{3,5},{1,3},{0,1},{10,8},{12,10},{14... | collective-permute-start | bytes 1572872 | tf_op jit(solution)/shard_map/ppermute | solution.py:52
  411.3 23.5 %collective-permute-start.33 = (bf16[512,512]{1,0:T(8,128)(2,1)}, bf16[512,512]{1,0:T(8,128)(2,1)}, u32[]{:S(2)}, u32[]{:S(2)}) collective-permute-start(bf16[512,512]{1,0:T(8,128)(2,1)} %collective-permute-done.29), channel_id=1, source_target_pairs={{0,2},{2,4},{4,6},{6,7},{7,5},{5,3},{3,1},{1,0},{8,10},{10,12},{12... | collective-permute-start | bytes 1572872 | tf_op jit(solution)/shard_map/ppermute | solution.py:52
  411.7 23.5 %collective-permute-start.34 = (bf16[512,512]{1,0:T(8,128)(2,1)S(1)}, bf16[512,512]{1,0:T(8,128)(2,1)}, u32[]{:S(2)}, u32[]{:S(2)}) collective-permute-start(bf16[512,512]{1,0:T(8,128)(2,1)S(1)} %collective-permute-done.30), channel_id=1, source_target_pairs={{2,0},{4,2},{6,4},{7,6},{5,7},{3,5},{1,3},{0,1},{10,8},{12,10},{14... | collective-permute-start | bytes 1572872 | tf_op jit(solution)/shard_map/ppermute | solution.py:52
  433.1 15.0 %collective-permute-start.36 = (bf16[512,512]{1,0:T(8,128)(2,1)}, bf16[512,512]{1,0:T(8,128)(2,1)S(1)}, u32[]{:S(2)}, u32[]{:S(2)}) collective-permute-start(bf16[512,512]{1,0:T(8,128)(2,1)} %collective-permute-done.32), channel_id=1, source_target_pairs={{2,0},{4,2},{6,4},{7,6},{5,7},{3,5},{1,3},{0,1},{10,8},{12,10},{14... | collective-permute-start | bytes 1572872 | tf_op jit(solution)/shard_map/ppermute | solution.py:52
  434.8 20.9 %collective-permute-start.37 = (bf16[512,512]{1,0:T(8,128)(2,1)}, bf16[512,512]{1,0:T(8,128)(2,1)S(1)}, u32[]{:S(2)}, u32[]{:S(2)}) collective-permute-start(bf16[512,512]{1,0:T(8,128)(2,1)} %collective-permute-done.33), channel_id=1, source_target_pairs={{0,2},{2,4},{4,6},{6,7},{7,5},{5,3},{3,1},{1,0},{8,10},{10,12},{12... | collective-permute-start | bytes 1572872 | tf_op jit(solution)/shard_map/ppermute | solution.py:52
  435.2 20.6 %collective-permute-start.38 = (bf16[512,512]{1,0:T(8,128)(2,1)}, bf16[512,512]{1,0:T(8,128)(2,1)}, u32[]{:S(2)}, u32[]{:S(2)}) collective-permute-start(bf16[512,512]{1,0:T(8,128)(2,1)} %collective-permute-done.34), channel_id=1, source_target_pairs={{2,0},{4,2},{6,4},{7,6},{5,7},{3,5},{1,3},{0,1},{10,8},{12,10},{14... | collective-permute-start | bytes 1572872 | tf_op jit(solution)/shard_map/ppermute | solution.py:52
  447.7 44.7 %collective-permute-start.45 = (bf16[1024,4096]{1,0:T(8,128)(2,1)}, bf16[1024,4096]{1,0:T(8,128)(2,1)}, u32[]{:S(2)}, u32[]{:S(2)}) collective-permute-start(bf16[1024,4096]{1,0:T(8,128)(2,1)} %all-gather.8.cloned.1.call-done.refs_0_.refs_1_), channel_id=1, source_target_pairs={{0,8},{8,0},{16,24},{24,16},{1,9},{9,1},{17,25},{25,17},{2,10},{10... | collective-permute-start | bytes 25165832 | tf_op jit(solution)/shard_map/ppermute | solution.py:418
  455.8 19.9 %collective-permute-start.39 = (bf16[512,512]{1,0:T(8,128)(2,1)}, bf16[512,512]{1,0:T(8,128)(2,1)S(1)}, u32[]{:S(2)}, u32[]{:S(2)}) collective-permute-start(bf16[512,512]{1,0:T(8,128)(2,1)} %collective-permute-done.35), channel_id=1, source_target_pairs={{0,2},{2,4},{4,6},{6,7},{7,5},{5,3},{3,1},{1,0},{8,10},{10,12},{12... | collective-permute-start | bytes 1572872 | tf_op jit(solution)/shard_map/ppermute | solution.py:52
  457.4 18.3 %collective-permute-start.40 = (bf16[512,512]{1,0:T(8,128)(2,1)}, bf16[512,512]{1,0:T(8,128)(2,1)S(1)}, u32[]{:S(2)}, u32[]{:S(2)}) collective-permute-start(bf16[512,512]{1,0:T(8,128)(2,1)} %collective-permute-done.38), channel_id=1, source_target_pairs={{2,0},{4,2},{6,4},{7,6},{5,7},{3,5},{1,3},{0,1},{10,8},{12,10},{14... | collective-permute-start | bytes 1572872 | tf_op jit(solution)/shard_map/ppermute | solution.py:52
  507.4 110.8 %collective-permute-start.48 = (bf16[3072,512]{1,0:T(8,128)(2,1)}, bf16[3072,512]{1,0:T(8,128)(2,1)}, u32[]{:S(2)}, u32[]{:S(2)}) collective-permute-start(bf16[3072,512]{1,0:T(8,128)(2,1)} %grad_rows.3), channel_id=1, source_target_pairs={{0,16},{8,24},{16,0},{24,8},{1,17},{9,25},{17,1},{25,9},{2,18},{10... | collective-permute-start | bytes 9437192 | tf_op jit(solution)/shard_map/ppermute | solution.py:474
  514.0 75.0 %collective-permute-start.41 = (f32[256,512]{1,0:T(8,128)S(1)}, f32[256,512]{1,0:T(8,128)}, u32[]{:S(2)}, u32[]{:S(2)}) collective-permute-start(f32[256,512]{1,0:T(8,128)S(1)} %get-tuple-element.65), channel_id=1, source_target_pairs={{0,24},{8,16},{16,8},{24,0},{1,25},{9,17},{17,9},{25,1},{2,26},{10... | collective-permute-start | bytes 1572872 | tf_op jit(solution)/shard_map/ppermute | solution.py:458
  514.0 86.1 %collective-permute-start.42 = (f32[256,512]{1,0:T(8,128)S(1)}, f32[256,512]{1,0:T(8,128)}, u32[]{:S(2)}, u32[]{:S(2)}) collective-permute-start(f32[256,512]{1,0:T(8,128)S(1)} %get-tuple-element.64), channel_id=1, source_target_pairs={{0,16},{8,24},{16,0},{24,8},{1,17},{9,25},{17,1},{25,9},{2,18},{10... | collective-permute-start | bytes 1572872 | tf_op jit(solution)/shard_map/ppermute | solution.py:458
  515.4 85.8 %collective-permute-start.43 = (f32[256,512]{1,0:T(8,128)S(1)}, f32[256,512]{1,0:T(8,128)}, u32[]{:S(2)}, u32[]{:S(2)}) collective-permute-start(f32[256,512]{1,0:T(8,128)S(1)} %get-tuple-element.63), channel_id=1, source_target_pairs={{0,8},{8,0},{16,24},{24,16},{1,9},{9,1},{17,25},{25,17},{2,10},{10... | collective-permute-start | bytes 1572872 | tf_op jit(solution)/shard_map/ppermute | solution.py:458
  (17 other events, 577.2 us)
Sparse Core Ops, SparseCore 0:
  9.5 117.5 all-gather.3
  128.7 137.2 all-gather.5
  267.5 136.0 all-gather.7

commit v2 on v1

--- a/solution.py
+++ b/solution.py
@@ -298,14 +298,15 @@
     )(places, table, *operands)
 
 
-def grad_rows(first, pieces, width, tables, feats, errors, out_dtype):
+def grad_rows(first, pieces, parts, width, tables, feats, errors, out_dtype):
     per = tables[0].shape[0]
     kinds = len(tables)
     tokens, cols = errors[0].shape
+    each = pieces // parts
 
     def body(first_ref, table_ref, *refs):
-        out_ref = refs[-1]
-        error_refs = refs[-1 - len(errors) : -1]
+        out_refs = refs[-parts:]
+        error_refs = refs[-parts - len(errors) : -parts]
         piece = first_ref[0] + pl.program_id(0)
         for at in range(kinds):
 
@@ -320,7 +321,14 @@
                         preferred_element_type=jnp.float32,
                     )
                     total = term if total is None else total + term
-                out_ref[...] = total.astype(out_dtype)
+                for part, out_ref in enumerate(out_refs):
+
+                    @pl.when(pl.program_id(0) // each == part)
+                    def _(out_ref=out_ref):
+                        out_ref[...] = total.astype(out_dtype)
+
+    def out_map(part):
+        return lambda i, first_ref, table_ref: (jnp.clip(i - part * each, 0, each - 1), 0)
 
     def feat_map(at):
         def of(i, first_ref, table_ref):
@@ -340,9 +348,9 @@
             num_scalar_prefetch=2,
             grid=(pieces,),
             in_specs=in_specs,
-            out_specs=pl.BlockSpec((width, cols), lambda i, first_ref, table_ref: (i, 0)),
-        ),
-        out_shape=jax.ShapeDtypeStruct((pieces * width, cols), out_dtype),
+            out_specs=[pl.BlockSpec((width, cols), out_map(part)) for part in range(parts)],
+        ),
+        out_shape=[jax.ShapeDtypeStruct((each * width, cols), out_dtype)] * parts,
         cost_estimate=pl.CostEstimate(
             flops=4 * tokens * pieces * width * cols,
             transcendentals=0,
@@ -350,6 +358,38 @@
         ),
         name="grad_rows",
     )(first.reshape(1), jnp.concatenate(tables), *[f for group in feats for f in group], *errors)
+
+
+def update(grads, far, joining, momentum, part, outs, tokens):
+    rows, cols = far[0].shape
+    step = math.gcd(rows, 256)
+    skip = part * (rows // step)
+
+    def body(grads_ref, joining_ref, momentum_ref, *refs):
+        total = grads_ref[...]
+        for far_ref in refs[: len(far)]:
+            total = total + far_ref[...].astype(jnp.float32)
+        fresh = mom_decay * momentum_ref[...] + total / tokens
+        refs[-2][...] = joining_ref[...] - step_size * fresh
+        refs[-1][...] = fresh
+
+    here = pl.BlockSpec((step, cols), lambda i: (skip + i, 0))
+    own = pl.BlockSpec((step, cols), lambda i: (i, 0))
+    shape = jax.ShapeDtypeStruct(joining.shape, jnp.float32)
+    return pl.pallas_call(
+        body,
+        grid=(rows // step,),
+        in_specs=[here] * 3
+        + [own] * len(far)
+        + [pl.BlockSpec(memory_space=pl.ANY)] * len(outs),
+        out_specs=[here, here],
+        out_shape=[shape, shape],
+        input_output_aliases={3 + len(far) + at: at for at in range(len(outs))},
+        cost_estimate=pl.CostEstimate(
+            flops=6 * rows * cols, transcendentals=0, bytes_accessed=22 * rows * cols
+        ),
+        name="update",
+    )(grads, joining, momentum, *far, *outs)
 
 
 def step_on_device(
@@ -454,6 +494,8 @@
     sent = []
     for k in sorted(range(groups), key=lambda k: -k):
         piece = lax.dynamic_slice_in_dim(error, inverse[mine ^ k] * block, block, 0)
+        if k > 1:
+            piece = piece.astype(jnp.bfloat16)
         if k:
             piece = lax.ppermute(piece, "wide", [(i, i ^ k) for i in range(groups)])
         sent.append((k, piece))
@@ -463,24 +505,39 @@
     feats = ((low_full, mid_full, high_full), (low_other, mid_other, high_other))
     per_chunk = rows_here // width
 
-    def rows_of(member, dtype):
+    def rows_of(member, parts, dtype):
         return grad_rows(
-            member * per_chunk, per_chunk, width, tables, feats, (error_bf, error_other), dtype
+            member * per_chunk,
+            per_chunk,
+            parts,
+            width,
+            tables,
+            feats,
+            (error_bf, error_other),
+            dtype,
         )
 
+    parts = 2
     far = []
     for bit in range(2, groups, 2):
-        away = rows_of(mine ^ bit, jnp.bfloat16)
-        far.append(lax.ppermute(away, "wide", [(i, i ^ bit) for i in range(groups)]))
-    grads = rows_of(mine, jnp.float32)
+        away = rows_of(mine ^ bit, parts, jnp.bfloat16)
+        moved = []
+        for piece in away:
+            moved.append(lax.ppermute(piece, "wide", [(i, i ^ bit) for i in range(groups)]))
+        far.append(moved)
+    (grads,) = rows_of(mine, 1, jnp.float32)
     error_out = jnp.zeros_like(error)
     for k, piece in sent:
-        error_out = lax.dynamic_update_slice(error_out, piece, ((mine ^ k) * block, 0))
-    for piece in far:
-        grads = grads + piece.astype(jnp.float32)
-    grads = grads / (tokens_local * groups)
-    new_momentum = mom_decay * momentum + grads
-    new_joining = joining_weight - step_size * new_momentum
+        error_out = lax.dynamic_update_slice(
+            error_out, piece.astype(jnp.float32), ((mine ^ k) * block, 0)
+        )
+    outs = ()
+    for part in range(parts):
+        pieces = [moved[part] for moved in far]
+        outs = update(
+            grads, pieces, joining_weight, momentum, part, outs, tokens_local * groups
+        )
+    new_joining, new_momentum = outs
     return (error_out, new_joining, new_momentum)
 
 

time: 640 us -> 626 us (0.978)
  waiting for transfers between devices: 329 us -> 305 us
  Pallas kernels: 95.6 us -> 112 us
  other arithmetic: 22.1 us -> 11.9 us
    pallas_call x0 -> x2, Pallas kernels: none -> 15.8 us  [update(): pl.pallas_call(body, grid=(rows // step,), in_specs=[here] * 3 + [own] *...]
    ppermute x3, waiting for transfers between devices: 82.2 us -> 68.8 us  [step_on_device(): piece = lax.ppermute(piece, 'wide', [(i, i ^ k) for i in range(groups)])]
    sub x1 -> x0, other arithmetic: 13.2 us -> none  [step_on_device(): new_joining = joining_weight - step_size * new_momentum]
  transfers between devices with their start and end apart: 53 -> 54, of which waited for: 23 -> 20; matrix products, arithmetic and copies ran while one was open for 17% -> 18% of each run, Pallas kernels for 13% -> 17%
where the time goes in v2:
time: 626 us; the launch traced here: 624 us
  waiting for transfers between devices  305 us (49%)
  Pallas kernels  112 us (18%)
  local copies, waits for them, and re-layouts  95.9 us (15%)
  starting transfers between devices  52.5 us (8%)
  between operations  38.1 us (6%)
  other arithmetic  11.9 us (2%)
  matrix products  8.24 us (1%)
    ppermute x28, waiting for transfers between devices, ring_gather(): got = lax.ppermute(moving[way, part], axis, back if way else ahead)  109 us
    ppermute x3, waiting for transfers between devices, step_on_device(): piece = lax.ppermute(piece, 'wide', [(i, i ^ k) for i in range(groups)])  68.8 us
    ppermute x9, waiting for transfers between devices, wide_pieces(): lax.ppermute(pieces[k & k - 1], axis, [(i, i ^ bit) for i in range(count)])  48.1 us
    all_gather x3, waiting for transfers between devices, listed_gather(): lax.all_gather(shard, axis, axis=1, tiled=True, axis_index_groups=[order])  44.1 us
    pallas_call x4, Pallas kernels, predict(): pl.pallas_call(body, grid_spec=pltpu.PrefetchScalarGridSpec(num_scalar_pr...  43.5 us
    dynamic_update_slice x28, local copies, waits for them, and re-layouts, ring_gather(): full = lax.dynamic_update_slice(full, got, (part * half, source * width))  36 us
    ppermute x4, waiting for transfers between devices, head_pieces(): got.append(lax.ppermute(part, axis, perm))  34.2 us
    pallas_call x2, Pallas kernels, grad_rows(): pl.pallas_call(body, grid_spec=pltpu.PrefetchScalarGridSpec(num_scalar_pr...  29.5 us
  transfers between devices with their start and end apart: 54, of which 20 were waited for; matrix products, arithmetic and copies ran while one was open for 18% of the time, Pallas kernels for 17%

profile of v2, /device:TPU:0, one launch (start us, length us, event | category | flops | bytes accessed | tf_op | source)
XLA Modules:
  0.0 623.7 jit_solution(12667885214887939649)
XLA Ops:
  8.7 4.9 convert_element_type.25
  13.6 3.0 collective-permute-start.8
  19.2 5.8 all-to-all-start
  25.8 5.7 collective-permute-start.1
  32.6 33.1 %collective-permute-done.1 = bf16[1024,64]{0,1:T(8,128)(2,1)S(1)} collective-permute-done((bf16[1024,64]{0,1:T(8,128)(2,1)S(1)}, bf16[1024,64]{0,1:T(8,128)(2,1)S(1)}, u32[]{:S(2)}, u32[]{:S(2)}) %collective-permute-start.1) | collective-permute-done | bytes 131104 | tf_op jit(solution)/shard_map/ppermute | solution.py:95
  65.7 19.3 %collective-permute-done.8 = bf16[3072,512]{1,0:T(8,128)(2,1)} collective-permute-done((bf16[3072,512]{1,0:T(8,128)(2,1)}, bf16[3072,512]{1,0:T(8,128)(2,1)}, u32[]{:S(2)}, u32[]{:S(2)}) %collective-permute-start.8) | collective-permute-done | bytes 3145760 | tf_op jit(solution)/shard_map/ppermute | solution.py:75
  95.2 18.7 %collective-permute-done.11 = bf16[1024,512]{1,0:T(8,128)(2,1)} collective-permute-done((bf16[1024,512]{1,0:T(8,128)(2,1)S(1)}, bf16[1024,512]{1,0:T(8,128)(2,1)}, u32[]{:S(2)}, u32[]{:S(2)}) %collective-permute-start.11) | collective-permute-done | bytes 1048608 | tf_op jit(solution)/shard_map/ppermute | solution.py:75
  113.9 9.6 %collective-permute-done.5 = bf16[1024,256]{1,0:T(8,128)(2,1)} collective-permute-done((bf16[1024,256]{1,0:T(8,128)(2,1)S(1)}, bf16[1024,256]{1,0:T(8,128)(2,1)}, u32[]{:S(2)}, u32[]{:S(2)}) %collective-permute-start.5) | collective-permute-done | bytes 524320 | tf_op jit(solution)/shard_map/ppermute | solution.py:75
  146.9 13.8 %project.1 = (bf16[1024,512]{1,0:T(8,128)(2,1)}, bf16[1024,128]{1,0:T(8,128)(2,1)}, bf16[1024,128]{1,0:T(8,128)(2,1)}) custom-call(bf16[1024,4096]{1,0:T(8,128)(2,1)} %all-gather.4.cloned.1.call-done.hidden_ref, f32[1,4096]{1,0:T(1,128)} %bitcast.87, bf16[4096,512]{1,0:T(8,128)(2,1)} %query_ref.1, bf16[4096,256]{1,0:T(8,128)(2,1)} %copy-done.5, ...), custom_call_target="tpu_custom_call" | custom-call | flops 6442450944 | bytes 8388608 | tf_op jit(solution)/shard_map/project/pallas_call | solution.py:138
  160.6 9.3 %attend.1 = bf16[1024,512]{1,0:T(8,128)(2,1)} custom-call(bf16[1024,512]{1,0:T(8,128)(2,1)} %get-tuple-element.39.q_ref, bf16[1024,128]{1,0:T(8,128)(2,1)} %get-tuple-element.40.k0_ref.k1_ref, bf16[1024,128]{1,0:T(8,128)(2,1)} %get-tuple-element.40.k0_ref.k1_ref, bf16[1024,128]{1,0:T(8,128)(2,1)} %get-tuple-element.41.v0_ref.v1_ref, ...), custom_call_target="tpu_custom_call" | custom-call | flops 4294967296 | bytes 2097152 | tf_op jit(solution)/shard_map/attend/pallas_call | solution.py:208
  175.3 2.3 constant_dynamic-update-slice_fusion.24
  177.7 2.5 broadcast_in_dim.34
  181.2 2.3 constant_dynamic-update-slice_fusion.11
  183.5 2.3 constant_dynamic-update-slice_fusion.10
  185.7 5.3 broadcast_in_dim.33
  191.0 3.7 constant_dynamic-update-slice_fusion.19
  194.7 3.8 constant_dynamic-update-slice_fusion.18
  198.6 3.8 constant_dynamic-update-slice_fusion.17
  202.4 2.3 constant_dynamic-update-slice_fusion.9
  204.6 3.9 constant_dynamic-update-slice_fusion.16.refs_1_
  210.5 9.2 %collective-permute-done.15 = bf16[512,512]{1,0:T(8,128)(2,1)S(1)} collective-permute-done((bf16[512,512]{1,0:T(8,128)(2,1)S(1)}, bf16[512,512]{1,0:T(8,128)(2,1)S(1)}, u32[]{:S(2)}, u32[]{:S(2)}) %collective-permute-start.15) | collective-permute-done | bytes 524320 | tf_op jit(solution)/shard_map/ppermute | solution.py:52
  221.8 44.1 %all-gather.6.cloned.1.call-done.refs_0_ = bf16[1024,4096]{1,0:T(8,128)(2,1)} async-done(((bf16[1024,512]{1,0:T(8,128)(2,1)}), bf16[1024,4096]{1,0:T(8,128)(2,1)}) %all-gather.6.cloned.1.call-update) | async-done | bytes 8388624 | tf_op jit(solution)/shard_map/all_gather | solution.py:67
  266.4 12.3 %predict.4.refs_2_ = f32[1024,512]{1,0:T(8,128)} custom-call(s32[8]{0:T(128)} %iota.19.places_ref, s32[8]{0:T(128)} %constant.215.clone.table_ref, bf16[1024,4096]{1,0:T(8,128)(2,1)} %all-gather.6.cloned.1.call-done.refs_0_, bf16[12288,512]{1,0:T(8,128)(2,1)} %constant_dynamic-update-slice_fusion.16.refs_1_), custom_call_target="tpu_custom_call" | custom-call | flops 4294967296 | bytes 8388608 | tf_op jit(solution)/shard_map/predict/pallas_call | solution.py:286
  287.2 1.9 constant_dynamic-update-slice_fusion.20
  289.1 1.9 constant_dynamic-update-slice_fusion.40
  291.0 15.6 %collective-permute-done.21 = bf16[512,512]{1,0:T(8,128)(2,1)S(1)} collective-permute-done((bf16[512,512]{1,0:T(8,128)(2,1)S(1)}, bf16[512,512]{1,0:T(8,128)(2,1)S(1)}, u32[]{:S(2)}, u32[]{:S(2)}) %collective-permute-start.21) | collective-permute-done | bytes 524320 | tf_op jit(solution)/shard_map/ppermute | solution.py:52
  307.6 21.1 %collective-permute-done.23 = bf16[512,512]{1,0:T(8,128)(2,1)S(1)} collective-permute-done((bf16[512,512]{1,0:T(8,128)(2,1)}, bf16[512,512]{1,0:T(8,128)(2,1)S(1)}, u32[]{:S(2)}, u32[]{:S(2)}) %collective-permute-start.23) | collective-permute-done | bytes 524320 | tf_op jit(solution)/shard_map/ppermute | solution.py:52
  335.8 18.8 %collective-permute-done.25 = bf16[512,512]{1,0:T(8,128)(2,1)S(1)} collective-permute-done((bf16[512,512]{1,0:T(8,128)(2,1)S(1)}, bf16[512,512]{1,0:T(8,128)(2,1)S(1)}, u32[]{:S(2)}, u32[]{:S(2)}) %collective-permute-start.25) | collective-permute-done | bytes 524320 | tf_op jit(solution)/shard_map/ppermute | solution.py:52
  357.6 8.2 %convert_add_fusion = f32[1024,512]{1,0:T(8,128)S(1)} fusion(bf16[1024,512]{1,0:T(8,128)(2,1)S(1)} %copy-done.7, bf16[1024,4096]{1,0:T(8,128)(2,1)} %constant_dynamic-update-slice_fusion.36, bf16[4096,512]{1,0:T(8,128)(2,1)} %bitcast.40), kind=kOutput, calls=%fused_computation.2 | convolution fusion | flops 4296015872 | bytes 15728640 | tf_op jit(solution)/shard_map/dot_general | solution.py:471
  379.3 15.2 %collective-permute-done.27 = bf16[512,512]{1,0:T(8,128)(2,1)} collective-permute-done((bf16[512,512]{1,0:T(8,128)(2,1)}, bf16[512,512]{1,0:T(8,128)(2,1)}, u32[]{:S(2)}, u32[]{:S(2)}) %collective-permute-start.27) | collective-permute-done | bytes 524320 | tf_op jit(solution)/shard_map/ppermute | solution.py:52
  396.5 15.0 %collective-permute-done.29 = bf16[512,512]{1,0:T(8,128)(2,1)} collective-permute-done((bf16[512,512]{1,0:T(8,128)(2,1)}, bf16[512,512]{1,0:T(8,128)(2,1)}, u32[]{:S(2)}, u32[]{:S(2)}) %collective-permute-start.29) | collective-permute-done | bytes 524320 | tf_op jit(solution)/shard_map/ppermute | solution.py:52
  414.1 13.1 %predict.5.refs_2_ = f32[1024,512]{1,0:T(8,128)} custom-call(s32[8]{0:T(128)} %iota.20.places_ref, s32[8]{0:T(128)} %constant.215.clone.table_ref, bf16[1024,4096]{1,0:T(8,128)(2,1)} %all-gather.8.cloned.1.call-done.refs_0_.refs_1_, bf16[12288,512]{1,0:T(8,128)(2,1)} %constant_dynamic-update-slice_fusion.16.refs_1_, f32[1024,512]{1,0:T(8,128)} %predict.4.refs_2_), custom_call_target="tpu_custom_call" | custom-call | flops 4294967296 | bytes 8388608 | tf_op jit(solution)/shard_map/predict/pallas_call | solution.py:286
  427.2 1.9 constant_dynamic-update-slice_fusion.7
  429.1 1.9 constant_dynamic-update-slice_fusion.6
  431.0 1.9 constant_dynamic-update-slice_fusion.35
  441.7 1.9 constant_dynamic-update-slice_fusion.33
  443.6 1.9 constant_dynamic-update-slice_fusion.32
  445.5 2.6 collective-permute-done.35
  448.3 7.8 %collective-permute-done.37 = bf16[512,512]{1,0:T(8,128)(2,1)S(1)} collective-permute-done((bf16[512,512]{1,0:T(8,128)(2,1)}, bf16[512,512]{1,0:T(8,128)(2,1)S(1)}, u32[]{:S(2)}, u32[]{:S(2)}) %collective-permute-start.37) | collective-permute-done | bytes 524320 | tf_op jit(solution)/shard_map/ppermute | solution.py:52
  458.2 2.0 constant_dynamic-update-slice_fusion.3
  461.8 2.0 constant_dynamic-update-slice_fusion.30.refs_0_
  463.8 12.1 %predict.6.refs_2_ = f32[1024,512]{1,0:T(8,128)} custom-call(s32[7]{0:T(128)} %pad_add_fusion.places_ref.table_ref, s32[7]{0:T(128)} %pad_add_fusion.places_ref.table_ref, bf16[1024,4096]{1,0:T(8,128)(2,1)} %constant_dynamic-update-slice_fusion.30.refs_0_, bf16[12288,512]{1,0:T(8,128)(2,1)} %constant_dynamic-update-slice_fusion.16.refs_1_, ...), custom_call_target="tpu_custom_call" | custom-call | flops 3758096384 | bytes 7340032 | tf_op jit(solution)/shard_map/predict/pallas_call | solution.py:286
  480.8 6.0 predict.7
  493.6 14.6 %grad_rows.3 = (bf16[1536,512]{1,0:T(8,128)(2,1)}, bf16[1536,512]{1,0:T(8,128)(2,1)}) custom-call(s32[1]{0:T(128)} %bitcast.56.first_ref, s32[24]{0:T(128)} %constant.219.table_ref, bf16[1024,4096]{1,0:T(8,128)(2,1)} %all-gather.6.cloned.1.call-done.refs_0_, bf16[1024,4096]{1,0:T(8,128)(2,1)} %all-gather.8.cloned.1.call-done.refs_0_.refs_1_, ...), custom_call_target="tpu_custom_call" | custom-call | flops 6442450944 | bytes 12582912 | tf_op jit(solution)/shard_map/grad_rows/pallas_call | solution.py:345
  515.4 68.8 %collective-permute-done.42 = bf16[256,512]{1,0:T(8,128)(2,1)} collective-permute-done((bf16[256,512]{1,0:T(8,128)(2,1)S(1)}, bf16[256,512]{1,0:T(8,128)(2,1)}, u32[]{:S(2)}, u32[]{:S(2)}) %collective-permute-start.42) | collective-permute-done | bytes 262176 | tf_op jit(solution)/shard_map/ppermute | solution.py:500
  586.4 15.0 %grad_rows.2.grads_ref = f32[3072,512]{1,0:T(8,128)} custom-call(s32[1]{0:T(128)} %bitcast.55.first_ref, s32[24]{0:T(128)} %constant.219.table_ref, bf16[1024,4096]{1,0:T(8,128)(2,1)} %all-gather.6.cloned.1.call-done.refs_0_, bf16[1024,4096]{1,0:T(8,128)(2,1)} %all-gather.8.cloned.1.call-done.refs_0_.refs_1_, ...), custom_call_target="tpu_custom_call" | custom-call | flops 6442450944 | bytes 12582912 | tf_op jit(solution)/shard_map/grad_rows/pallas_call | solution.py:345
  601.4 7.9 %update.2 = (f32[3072,512]{1,0:T(8,128)}, f32[3072,512]{1,0:T(8,128)}) custom-call(f32[3072,512]{1,0:T(8,128)} %grad_rows.2.grads_ref, f32[3072,512]{1,0:T(8,128)} %joining_ref.3, f32[3072,512]{1,0:T(8,128)} %momentum_ref.3, bf16[1536,512]{1,0:T(8,128)(2,1)} %collective-permute-done.49.refs_0_), custom_call_target="tpu_custom_call" | custom-call | flops 4718592 | bytes 17301504 | tf_op jit(solution)/shard_map/update/pallas_call | solution.py:379
  609.3 7.9 %update.3 = (f32[3072,512]{1,0:T(8,128)}, f32[3072,512]{1,0:T(8,128)}) custom-call(f32[3072,512]{1,0:T(8,128)} %grad_rows.2.grads_ref, f32[3072,512]{1,0:T(8,128)} %joining_ref.3, f32[3072,512]{1,0:T(8,128)} %momentum_ref.3, bf16[1536,512]{1,0:T(8,128)(2,1)} %collective-permute-done.48.refs_0_, ...), custom_call_target="tpu_custom_call", output_to_operand_aliasing={{0}: (4, {}), {1}: (5, {})} | custom-call | flops 4718592 | bytes 17301504 | tf_op jit(solution)/shard_map/update/pallas_call | solution.py:379
  (189 shorter events, 97.8 us)
Async XLA Ops:
  7.2 138.4 %all-gather.4.cloned.1.call-start = ((), (), s32[]{:S(2)}) async-start(), calls=%async_computation.1 | async-start | bytes 9437184 | tf_op jit(solution)/shard_map/all_gather | solution.py:67
  7.9 258.0 %all-gather.6.cloned.1.call-start = ((), (), s32[]{:S(2)}) async-start(), calls=%async_computation.2 | async-start | bytes 9437184 | tf_op jit(solution)/shard_map/all_gather | solution.py:67
  8.7 404.9 %all-gather.8.cloned.1.call-start = ((), (), s32[]{:S(2)}) async-start(), calls=%async_computation.3 | async-start | bytes 9437184 | tf_op jit(solution)/shard_map/all_gather | solution.py:67
  13.6 71.4 %collective-permute-start.8 = (bf16[3072,512]{1,0:T(8,128)(2,1)}, bf16[3072,512]{1,0:T(8,128)(2,1)}, u32[]{:S(2)}, u32[]{:S(2)}) collective-permute-start(bf16[3072,512]{1,0:T(8,128)(2,1)} %convert_element_type.25), channel_id=1, source_target_pairs={{0,16},{8,24},{16,0},{24,8},{1,17},{9,25},{17,1},{25,9},{2,18},{10... | collective-permute-start | bytes 9437192 | tf_op jit(solution)/shard_map/ppermute | solution.py:75
  19.2 67.0 %all-to-all-start = ((bf16[128,8,512]{0,2,1:T(8,128)(2,1)}), bf16[128,8,512]{0,2,1:T(8,128)(2,1)S(1)}, u32[]{:S(2)}, u32[]{:S(2)}) async-start(bf16[128,8,512]{0,2,1:T(8,128)(2,1)} %bitcast.10), calls=%async_computation | async-start | bytes 2097152 | tf_op jit(solution)/shard_map/all_to_all | solution.py:425
  25.8 39.9 %collective-permute-start.1 = (bf16[1024,64]{0,1:T(8,128)(2,1)S(1)}, bf16[1024,64]{0,1:T(8,128)(2,1)S(1)}, u32[]{:S(2)}, u32[]{:S(2)}) collective-permute-start(bf16[1024,64]{0,1:T(8,128)(2,1)S(1)} %constant_dynamic-slice_fusion.5), channel_id=1, source_target_pairs={{1,0},{4,1},{5,2},{0,3},{3,4},{6,5},{7,6},{2,7},{9,8},{12,9},{13,1... | collective-permute-start | bytes 393224 | tf_op jit(solution)/shard_map/ppermute | solution.py:95
  31.4 53.5 %collective-permute-start.2 = (bf16[1024,64]{0,1:T(8,128)(2,1)S(1)}, bf16[1024,64]{0,1:T(8,128)(2,1)S(1)}, u32[]{:S(2)}, u32[]{:S(2)}) collective-permute-start(bf16[1024,64]{0,1:T(8,128)(2,1)S(1)} %constant_dynamic-slice_fusion.5), channel_id=1, source_target_pairs={{4,0},{5,1},{0,2},{1,3},{6,4},{7,5},{2,6},{3,7},{12,8},{13,9},{8,1... | collective-permute-start | bytes 393224 | tf_op jit(solution)/shard_map/ppermute | solution.py:95
  31.4 54.7 %collective-permute-start.3 = (bf16[1024,64]{0,1:T(8,128)(2,1)S(1)}, bf16[1024,64]{0,1:T(8,128)(2,1)S(1)}, u32[]{:S(2)}, u32[]{:S(2)}) collective-permute-start(bf16[1024,64]{0,1:T(8,128)(2,1)S(1)} %constant_dynamic-slice_fusion.5), channel_id=1, source_target_pairs={{5,0},{0,1},{1,2},{4,3},{7,4},{2,5},{3,6},{6,7},{13,8},{8,9},{9,10... | collective-permute-start | bytes 393224 | tf_op jit(solution)/shard_map/ppermute | solution.py:95
  32.5 113.0 %collective-permute-start.7 = (bf16[3072,512]{1,0:T(8,128)(2,1)}, bf16[3072,512]{1,0:T(8,128)(2,1)}, u32[]{:S(2)}, u32[]{:S(2)}) collective-permute-start(bf16[3072,512]{1,0:T(8,128)(2,1)} %convert_element_type.25), channel_id=1, source_target_pairs={{0,8},{8,0},{16,24},{24,16},{1,9},{9,1},{17,25},{25,17},{2,10},{10... | collective-permute-start | bytes 9437192 | tf_op jit(solution)/shard_map/ppermute | solution.py:75
  84.9 60.6 %collective-permute-start.9 = (bf16[3072,512]{1,0:T(8,128)(2,1)}, bf16[3072,512]{1,0:T(8,128)(2,1)}, u32[]{:S(2)}, u32[]{:S(2)}) collective-permute-start(bf16[3072,512]{1,0:T(8,128)(2,1)} %collective-permute-done.8), channel_id=1, source_target_pairs={{0,8},{8,0},{16,24},{24,16},{1,9},{9,1},{17,25},{25,17},{2,10},{10... | collective-permute-start | bytes 9437192 | tf_op jit(solution)/shard_map/ppermute | solution.py:75
  87.7 26.2 %collective-permute-start.11 = (bf16[1024,512]{1,0:T(8,128)(2,1)S(1)}, bf16[1024,512]{1,0:T(8,128)(2,1)}, u32[]{:S(2)}, u32[]{:S(2)}) collective-permute-start(bf16[1024,512]{1,0:T(8,128)(2,1)S(1)} %bitcast.76), channel_id=1, source_target_pairs={{0,16},{8,24},{16,0},{24,8},{1,17},{9,25},{17,1},{25,9},{2,18},{10... | collective-permute-start | bytes 3145736 | tf_op jit(solution)/shard_map/ppermute | solution.py:75
  93.3 30.3 %collective-permute-start.5 = (bf16[1024,256]{1,0:T(8,128)(2,1)S(1)}, bf16[1024,256]{1,0:T(8,128)(2,1)}, u32[]{:S(2)}, u32[]{:S(2)}) collective-permute-start(bf16[1024,256]{1,0:T(8,128)(2,1)S(1)} %get-tuple-element.81), channel_id=1, source_target_pairs={{0,16},{8,24},{16,0},{24,8},{1,17},{9,25},{17,1},{25,9},{2,18},{10... | collective-permute-start | bytes 1572872 | tf_op jit(solution)/shard_map/ppermute | solution.py:75
  94.9 50.6 %collective-permute-start.10 = (bf16[1024,512]{1,0:T(8,128)(2,1)S(1)}, bf16[1024,512]{1,0:T(8,128)(2,1)}, u32[]{:S(2)}, u32[]{:S(2)}) collective-permute-start(bf16[1024,512]{1,0:T(8,128)(2,1)S(1)} %bitcast.77), channel_id=1, source_target_pairs={{0,8},{8,0},{16,24},{24,16},{1,9},{9,1},{17,25},{25,17},{2,10},{10... | collective-permute-start | bytes 3145736 | tf_op jit(solution)/shard_map/ppermute | solution.py:75
  113.9 31.7 %collective-permute-start.12 = (bf16[1024,512]{1,0:T(8,128)(2,1)}, bf16[1024,512]{1,0:T(8,128)(2,1)}, u32[]{:S(2)}, u32[]{:S(2)}) collective-permute-start(bf16[1024,512]{1,0:T(8,128)(2,1)} %collective-permute-done.11), channel_id=1, source_target_pairs={{0,8},{8,0},{16,24},{24,16},{1,9},{9,1},{17,25},{25,17},{2,10},{10... | collective-permute-start | bytes 3145736 | tf_op jit(solution)/shard_map/ppermute | solution.py:75
  123.5 20.9 %collective-permute-start.6 = (bf16[1024,256]{1,0:T(8,128)(2,1)}, bf16[1024,256]{1,0:T(8,128)(2,1)}, u32[]{:S(2)}, u32[]{:S(2)}) collective-permute-start(bf16[1024,256]{1,0:T(8,128)(2,1)} %collective-permute-done.5), channel_id=1, source_target_pairs={{0,8},{8,0},{16,24},{24,16},{1,9},{9,1},{17,25},{25,17},{2,10},{10... | collective-permute-start | bytes 1572872 | tf_op jit(solution)/shard_map/ppermute | solution.py:75
  171.2 37.3 %collective-permute-start.13 = (bf16[512,512]{1,0:T(8,128)(2,1)S(1)}, bf16[512,512]{1,0:T(8,128)(2,1)S(1)}, u32[]{:S(2)}, u32[]{:S(2)}) collective-permute-start(bf16[512,512]{1,0:T(8,128)(2,1)S(1)} %get-tuple-element.78), channel_id=1, source_target_pairs={{0,2},{2,4},{4,6},{6,7},{7,5},{5,3},{3,1},{1,0},{8,10},{10,12},{12... | collective-permute-start | bytes 1572872 | tf_op jit(solution)/shard_map/ppermute | solution.py:52
  173.1 37.3 %collective-permute-start.14 = (bf16[512,512]{1,0:T(8,128)(2,1)S(1)}, bf16[512,512]{1,0:T(8,128)(2,1)S(1)}, u32[]{:S(2)}, u32[]{:S(2)}) collective-permute-start(bf16[512,512]{1,0:T(8,128)(2,1)S(1)} %get-tuple-element.78), channel_id=1, source_target_pairs={{2,0},{4,2},{6,4},{7,6},{5,7},{3,5},{1,3},{0,1},{10,8},{12,10},{14... | collective-permute-start | bytes 1572872 | tf_op jit(solution)/shard_map/ppermute | solution.py:52
  173.3 46.5 %collective-permute-start.15 = (bf16[512,512]{1,0:T(8,128)(2,1)S(1)}, bf16[512,512]{1,0:T(8,128)(2,1)S(1)}, u32[]{:S(2)}, u32[]{:S(2)}) collective-permute-start(bf16[512,512]{1,0:T(8,128)(2,1)S(1)} %get-tuple-element.77), channel_id=1, source_target_pairs={{0,2},{2,4},{4,6},{6,7},{7,5},{5,3},{3,1},{1,0},{8,10},{10,12},{12... | collective-permute-start | bytes 1572872 | tf_op jit(solution)/shard_map/ppermute | solution.py:52
  175.1 46.5 %collective-permute-start.16 = (bf16[512,512]{1,0:T(8,128)(2,1)S(1)}, bf16[512,512]{1,0:T(8,128)(2,1)S(1)}, u32[]{:S(2)}, u32[]{:S(2)}) collective-permute-start(bf16[512,512]{1,0:T(8,128)(2,1)S(1)} %get-tuple-element.77), channel_id=1, source_target_pairs={{2,0},{4,2},{6,4},{7,6},{5,7},{3,5},{1,3},{0,1},{10,8},{12,10},{14... | collective-permute-start | bytes 1572872 | tf_op jit(solution)/shard_map/ppermute | solution.py:52
  208.5 72.0 %collective-permute-start.17 = (bf16[512,512]{1,0:T(8,128)(2,1)S(1)}, bf16[512,512]{1,0:T(8,128)(2,1)S(1)}, u32[]{:S(2)}, u32[]{:S(2)}) collective-permute-start(bf16[512,512]{1,0:T(8,128)(2,1)S(1)} %collective-permute-done.13), channel_id=1, source_target_pairs={{0,2},{2,4},{4,6},{6,7},{7,5},{5,3},{3,1},{1,0},{8,10},{10,12},{12... | collective-permute-start | bytes 1572872 | tf_op jit(solution)/shard_map/ppermute | solution.py:52
  210.4 70.9 %collective-permute-start.18 = (bf16[512,512]{1,0:T(8,128)(2,1)S(1)}, bf16[512,512]{1,0:T(8,128)(2,1)}, u32[]{:S(2)}, u32[]{:S(2)}) collective-permute-start(bf16[512,512]{1,0:T(8,128)(2,1)S(1)} %collective-permute-done.14), channel_id=1, source_target_pairs={{2,0},{4,2},{6,4},{7,6},{5,7},{3,5},{1,3},{0,1},{10,8},{12,10},{14... | collective-permute-start | bytes 1572872 | tf_op jit(solution)/shard_map/ppermute | solution.py:52
  219.8 62.8 %collective-permute-start.19 = (bf16[512,512]{1,0:T(8,128)(2,1)S(1)}, bf16[512,512]{1,0:T(8,128)(2,1)}, u32[]{:S(2)}, u32[]{:S(2)}) collective-permute-start(bf16[512,512]{1,0:T(8,128)(2,1)S(1)} %collective-permute-done.15), channel_id=1, source_target_pairs={{0,2},{2,4},{4,6},{6,7},{7,5},{5,3},{3,1},{1,0},{8,10},{10,12},{12... | collective-permute-start | bytes 1572872 | tf_op jit(solution)/shard_map/ppermute | solution.py:52
  221.6 61.8 %collective-permute-start.20 = (bf16[512,512]{1,0:T(8,128)(2,1)S(1)}, bf16[512,512]{1,0:T(8,128)(2,1)S(1)}, u32[]{:S(2)}, u32[]{:S(2)}) collective-permute-start(bf16[512,512]{1,0:T(8,128)(2,1)S(1)} %collective-permute-done.16), channel_id=1, source_target_pairs={{2,0},{4,2},{6,4},{7,6},{5,7},{3,5},{1,3},{0,1},{10,8},{12,10},{14... | collective-permute-start | bytes 1572872 | tf_op jit(solution)/shard_map/ppermute | solution.py:52
  280.6 26.0 %collective-permute-start.21 = (bf16[512,512]{1,0:T(8,128)(2,1)S(1)}, bf16[512,512]{1,0:T(8,128)(2,1)S(1)}, u32[]{:S(2)}, u32[]{:S(2)}) collective-permute-start(bf16[512,512]{1,0:T(8,128)(2,1)S(1)} %collective-permute-done.17), channel_id=1, source_target_pairs={{0,2},{2,4},{4,6},{6,7},{7,5},{5,3},{3,1},{1,0},{8,10},{10,12},{12... | collective-permute-start | bytes 1572872 | tf_op jit(solution)/shard_map/ppermute | solution.py:52
  281.3 26.2 %collective-permute-start.22 = (bf16[512,512]{1,0:T(8,128)(2,1)}, bf16[512,512]{1,0:T(8,128)(2,1)S(1)}, u32[]{:S(2)}, u32[]{:S(2)}) collective-permute-start(bf16[512,512]{1,0:T(8,128)(2,1)} %collective-permute-done.18), channel_id=1, source_target_pairs={{2,0},{4,2},{6,4},{7,6},{5,7},{3,5},{1,3},{0,1},{10,8},{12,10},{14... | collective-permute-start | bytes 1572872 | tf_op jit(solution)/shard_map/ppermute | solution.py:52
  282.6 46.0 %collective-permute-start.23 = (bf16[512,512]{1,0:T(8,128)(2,1)}, bf16[512,512]{1,0:T(8,128)(2,1)S(1)}, u32[]{:S(2)}, u32[]{:S(2)}) collective-permute-start(bf16[512,512]{1,0:T(8,128)(2,1)} %collective-permute-done.19), channel_id=1, source_target_pairs={{0,2},{2,4},{4,6},{6,7},{7,5},{5,3},{3,1},{1,0},{8,10},{10,12},{12... | collective-permute-start | bytes 1572872 | tf_op jit(solution)/shard_map/ppermute | solution.py:52
  283.4 46.0 %collective-permute-start.24 = (bf16[512,512]{1,0:T(8,128)(2,1)S(1)}, bf16[512,512]{1,0:T(8,128)(2,1)S(1)}, u32[]{:S(2)}, u32[]{:S(2)}) collective-permute-start(bf16[512,512]{1,0:T(8,128)(2,1)S(1)} %collective-permute-done.20), channel_id=1, source_target_pairs={{2,0},{4,2},{6,4},{7,6},{5,7},{3,5},{1,3},{0,1},{10,8},{12,10},{14... | collective-permute-start | bytes 1572872 | tf_op jit(solution)/shard_map/ppermute | solution.py:52
  329.4 25.2 %collective-permute-start.25 = (bf16[512,512]{1,0:T(8,128)(2,1)S(1)}, bf16[512,512]{1,0:T(8,128)(2,1)S(1)}, u32[]{:S(2)}, u32[]{:S(2)}) collective-permute-start(bf16[512,512]{1,0:T(8,128)(2,1)S(1)} %collective-permute-done.21), channel_id=1, source_target_pairs={{0,2},{2,4},{4,6},{6,7},{7,5},{5,3},{3,1},{1,0},{8,10},{10,12},{12... | collective-permute-start | bytes 1572872 | tf_op jit(solution)/shard_map/ppermute | solution.py:52
  331.7 25.1 %collective-permute-start.26 = (bf16[512,512]{1,0:T(8,128)(2,1)S(1)}, bf16[512,512]{1,0:T(8,128)(2,1)S(1)}, u32[]{:S(2)}, u32[]{:S(2)}) collective-permute-start(bf16[512,512]{1,0:T(8,128)(2,1)S(1)} %collective-permute-done.24), channel_id=1, source_target_pairs={{2,0},{4,2},{6,4},{7,6},{5,7},{3,5},{1,3},{0,1},{10,8},{12,10},{14... | collective-permute-start | bytes 1572872 | tf_op jit(solution)/shard_map/ppermute | solution.py:52
  368.1 26.3 %collective-permute-start.27 = (bf16[512,512]{1,0:T(8,128)(2,1)}, bf16[512,512]{1,0:T(8,128)(2,1)}, u32[]{:S(2)}, u32[]{:S(2)}) collective-permute-start(bf16[512,512]{1,0:T(8,128)(2,1)} %get-tuple-element.76), channel_id=1, source_target_pairs={{0,2},{2,4},{4,6},{6,7},{7,5},{5,3},{3,1},{1,0},{8,10},{10,12},{12... | collective-permute-start | bytes 1572872 | tf_op jit(solution)/shard_map/ppermute | solution.py:52
  369.5 26.4 %collective-permute-start.28 = (bf16[512,512]{1,0:T(8,128)(2,1)}, bf16[512,512]{1,0:T(8,128)(2,1)}, u32[]{:S(2)}, u32[]{:S(2)}) collective-permute-start(bf16[512,512]{1,0:T(8,128)(2,1)} %get-tuple-element.76), channel_id=1, source_target_pairs={{2,0},{4,2},{6,4},{7,6},{5,7},{3,5},{1,3},{0,1},{10,8},{12,10},{14... | collective-permute-start | bytes 1572872 | tf_op jit(solution)/shard_map/ppermute | solution.py:52
  370.2 41.4 %collective-permute-start.29 = (bf16[512,512]{1,0:T(8,128)(2,1)}, bf16[512,512]{1,0:T(8,128)(2,1)}, u32[]{:S(2)}, u32[]{:S(2)}) collective-permute-start(bf16[512,512]{1,0:T(8,128)(2,1)} %get-tuple-element.75), channel_id=1, source_target_pairs={{0,2},{2,4},{4,6},{6,7},{7,5},{5,3},{3,1},{1,0},{8,10},{10,12},{12... | collective-permute-start | bytes 1572872 | tf_op jit(solution)/shard_map/ppermute | solution.py:52
  371.5 40.3 %collective-permute-start.30 = (bf16[512,512]{1,0:T(8,128)(2,1)}, bf16[512,512]{1,0:T(8,128)(2,1)S(1)}, u32[]{:S(2)}, u32[]{:S(2)}) collective-permute-start(bf16[512,512]{1,0:T(8,128)(2,1)} %get-tuple-element.75), channel_id=1, source_target_pairs={{2,0},{4,2},{6,4},{7,6},{5,7},{3,5},{1,3},{0,1},{10,8},{12,10},{14... | collective-permute-start | bytes 1572872 | tf_op jit(solution)/shard_map/ppermute | solution.py:52
  379.3 113.3 %collective-permute-start.44 = (bf16[1024,4096]{1,0:T(8,128)(2,1)}, bf16[1024,4096]{1,0:T(8,128)(2,1)}, u32[]{:S(2)}, u32[]{:S(2)}) collective-permute-start(bf16[1024,4096]{1,0:T(8,128)(2,1)} %all-gather.6.cloned.1.call-done.refs_0_), channel_id=1, source_target_pairs={{0,8},{8,0},{16,24},{24,16},{1,9},{9,1},{17,25},{25,17},{2,10},{10... | collective-permute-start | bytes 25165832 | tf_op jit(solution)/shard_map/ppermute | solution.py:457
  394.5 38.5 %collective-permute-start.31 = (bf16[512,512]{1,0:T(8,128)(2,1)}, bf16[512,512]{1,0:T(8,128)(2,1)}, u32[]{:S(2)}, u32[]{:S(2)}) collective-permute-start(bf16[512,512]{1,0:T(8,128)(2,1)} %collective-permute-done.27), channel_id=1, source_target_pairs={{0,2},{2,4},{4,6},{6,7},{7,5},{5,3},{3,1},{1,0},{8,10},{10,12},{12... | collective-permute-start | bytes 1572872 | tf_op jit(solution)/shard_map/ppermute | solution.py:52
  395.9 37.4 %collective-permute-start.32 = (bf16[512,512]{1,0:T(8,128)(2,1)}, bf16[512,512]{1,0:T(8,128)(2,1)}, u32[]{:S(2)}, u32[]{:S(2)}) collective-permute-start(bf16[512,512]{1,0:T(8,128)(2,1)} %collective-permute-done.28), channel_id=1, source_target_pairs={{2,0},{4,2},{6,4},{7,6},{5,7},{3,5},{1,3},{0,1},{10,8},{12,10},{14... | collective-permute-start | bytes 1572872 | tf_op jit(solution)/shard_map/ppermute | solution.py:52
  411.5 23.4 %collective-permute-start.33 = (bf16[512,512]{1,0:T(8,128)(2,1)}, bf16[512,512]{1,0:T(8,128)(2,1)}, u32[]{:S(2)}, u32[]{:S(2)}) collective-permute-start(bf16[512,512]{1,0:T(8,128)(2,1)} %collective-permute-done.29), channel_id=1, source_target_pairs={{0,2},{2,4},{4,6},{6,7},{7,5},{5,3},{3,1},{1,0},{8,10},{10,12},{12... | collective-permute-start | bytes 1572872 | tf_op jit(solution)/shard_map/ppermute | solution.py:52
  411.9 23.5 %collective-permute-start.34 = (bf16[512,512]{1,0:T(8,128)(2,1)S(1)}, bf16[512,512]{1,0:T(8,128)(2,1)}, u32[]{:S(2)}, u32[]{:S(2)}) collective-permute-start(bf16[512,512]{1,0:T(8,128)(2,1)S(1)} %collective-permute-done.30), channel_id=1, source_target_pairs={{2,0},{4,2},{6,4},{7,6},{5,7},{3,5},{1,3},{0,1},{10,8},{12,10},{14... | collective-permute-start | bytes 1572872 | tf_op jit(solution)/shard_map/ppermute | solution.py:52
  435.0 21.1 %collective-permute-start.37 = (bf16[512,512]{1,0:T(8,128)(2,1)}, bf16[512,512]{1,0:T(8,128)(2,1)S(1)}, u32[]{:S(2)}, u32[]{:S(2)}) collective-permute-start(bf16[512,512]{1,0:T(8,128)(2,1)} %collective-permute-done.33), channel_id=1, source_target_pairs={{0,2},{2,4},{4,6},{6,7},{7,5},{5,3},{3,1},{1,0},{8,10},{10,12},{12... | collective-permute-start | bytes 1572872 | tf_op jit(solution)/shard_map/ppermute | solution.py:52
  435.4 20.8 %collective-permute-start.38 = (bf16[512,512]{1,0:T(8,128)(2,1)}, bf16[512,512]{1,0:T(8,128)(2,1)}, u32[]{:S(2)}, u32[]{:S(2)}) collective-permute-start(bf16[512,512]{1,0:T(8,128)(2,1)} %collective-permute-done.34), channel_id=1, source_target_pairs={{2,0},{4,2},{6,4},{7,6},{5,7},{3,5},{1,3},{0,1},{10,8},{12,10},{14... | collective-permute-start | bytes 1572872 | tf_op jit(solution)/shard_map/ppermute | solution.py:52
  448.1 44.5 %collective-permute-start.45 = (bf16[1024,4096]{1,0:T(8,128)(2,1)}, bf16[1024,4096]{1,0:T(8,128)(2,1)}, u32[]{:S(2)}, u32[]{:S(2)}) collective-permute-start(bf16[1024,4096]{1,0:T(8,128)(2,1)} %all-gather.8.cloned.1.call-done.refs_0_.refs_1_), channel_id=1, source_target_pairs={{0,8},{8,0},{16,24},{24,16},{1,9},{9,1},{17,25},{25,17},{2,10},{10... | collective-permute-start | bytes 25165832 | tf_op jit(solution)/shard_map/ppermute | solution.py:458
  456.1 19.7 %collective-permute-start.39 = (bf16[512,512]{1,0:T(8,128)(2,1)}, bf16[512,512]{1,0:T(8,128)(2,1)S(1)}, u32[]{:S(2)}, u32[]{:S(2)}) collective-permute-start(bf16[512,512]{1,0:T(8,128)(2,1)} %collective-permute-done.35), channel_id=1, source_target_pairs={{0,2},{2,4},{4,6},{6,7},{7,5},{5,3},{3,1},{1,0},{8,10},{10,12},{12... | collective-permute-start | bytes 1572872 | tf_op jit(solution)/shard_map/ppermute | solution.py:52
  457.4 18.5 %collective-permute-start.40 = (bf16[512,512]{1,0:T(8,128)(2,1)}, bf16[512,512]{1,0:T(8,128)(2,1)S(1)}, u32[]{:S(2)}, u32[]{:S(2)}) collective-permute-start(bf16[512,512]{1,0:T(8,128)(2,1)} %collective-permute-done.38), channel_id=1, source_target_pairs={{2,0},{4,2},{6,4},{7,6},{5,7},{3,5},{1,3},{0,1},{10,8},{12,10},{14... | collective-permute-start | bytes 1572872 | tf_op jit(solution)/shard_map/ppermute | solution.py:52
  491.4 22.7 %collective-permute-start.41 = (bf16[256,512]{1,0:T(8,128)(2,1)S(1)}, bf16[256,512]{1,0:T(8,128)(2,1)}, u32[]{:S(2)}, u32[]{:S(2)}) collective-permute-start(bf16[256,512]{1,0:T(8,128)(2,1)S(1)} %get-tuple-element.74), channel_id=1, source_target_pairs={{0,24},{8,16},{16,8},{24,0},{1,25},{9,17},{17,9},{25,1},{2,26},{10... | collective-permute-start | bytes 786440 | tf_op jit(solution)/shard_map/ppermute | solution.py:500
  508.1 93.3 %collective-permute-start.49 = (bf16[1536,512]{1,0:T(8,128)(2,1)}, bf16[1536,512]{1,0:T(8,128)(2,1)}, u32[]{:S(2)}, u32[]{:S(2)}) collective-permute-start(bf16[1536,512]{1,0:T(8,128)(2,1)} %get-tuple-element.66), channel_id=1, source_target_pairs={{0,16},{8,24},{16,0},{24,8},{1,17},{9,25},{17,1},{25,9},{2,18},{10... | collective-permute-start | bytes 4718600 | tf_op jit(solution)/shard_map/ppermute | solution.py:526
  509.5 99.7 %collective-permute-start.48 = (bf16[1536,512]{1,0:T(8,128)(2,1)}, bf16[1536,512]{1,0:T(8,128)(2,1)}, u32[]{:S(2)}, u32[]{:S(2)}) collective-permute-start(bf16[1536,512]{1,0:T(8,128)(2,1)} %get-tuple-element.65), channel_id=1, source_target_pairs={{0,16},{8,24},{16,0},{24,8},{1,17},{9,25},{17,1},{25,9},{2,18},{10... | collective-permute-start | bytes 4718600 | tf_op jit(solution)/shard_map/ppermute | solution.py:526
  511.9 73.3 %collective-permute-start.43 = (f32[256,512]{1,0:T(8,128)S(1)}, f32[256,512]{1,0:T(8,128)S(1)}, u32[]{:S(2)}, u32[]{:S(2)}) collective-permute-start(f32[256,512]{1,0:T(8,128)S(1)} %constant_dynamic-slice_fusion.1), channel_id=1, source_target_pairs={{0,8},{8,0},{16,24},{24,16},{1,9},{9,1},{17,25},{25,17},{2,10},{10... | collective-permute-start | bytes 1572872 | tf_op jit(solution)/shard_map/ppermute | solution.py:500
  512.0 72.3 %collective-permute-start.42 = (bf16[256,512]{1,0:T(8,128)(2,1)S(1)}, bf16[256,512]{1,0:T(8,128)(2,1)}, u32[]{:S(2)}, u32[]{:S(2)}) collective-permute-start(bf16[256,512]{1,0:T(8,128)(2,1)S(1)} %get-tuple-element.73), channel_id=1, source_target_pairs={{0,16},{8,24},{16,0},{24,8},{1,17},{9,25},{17,1},{25,9},{2,18},{10... | collective-permute-start | bytes 786440 | tf_op jit(solution)/shard_map/ppermute | solution.py:500
  (19 other events, 597.0 us)
Sparse Core Ops, SparseCore 0:
  9.5 117.5 all-gather.3
  128.7 137.2 all-gather.5
  267.5 139.4 all-gather.7

commit v3 on v2

--- a/solution.py
+++ b/solution.py
@@ -505,27 +505,29 @@
     feats = ((low_full, mid_full, high_full), (low_other, mid_other, high_other))
     per_chunk = rows_here // width
 
-    def rows_of(member, parts, dtype):
-        return grad_rows(
-            member * per_chunk,
-            per_chunk,
-            parts,
+    def rows_of(member, start, pieces, dtype):
+        (rows,) = grad_rows(
+            member * per_chunk + start,
+            pieces,
+            1,
             width,
             tables,
             feats,
             (error_bf, error_other),
             dtype,
         )
+        return rows
 
     parts = 2
+    each = per_chunk // parts
     far = []
     for bit in range(2, groups, 2):
-        away = rows_of(mine ^ bit, parts, jnp.bfloat16)
         moved = []
-        for piece in away:
-            moved.append(lax.ppermute(piece, "wide", [(i, i ^ bit) for i in range(groups)]))
+        for part in range(parts):
+            away = rows_of(mine ^ bit, part * each, each, jnp.bfloat16)
+            moved.append(lax.ppermute(away, "wide", [(i, i ^ bit) for i in range(groups)]))
         far.append(moved)
-    (grads,) = rows_of(mine, 1, jnp.float32)
+    grads = rows_of(mine, 0, per_chunk, jnp.float32)
     error_out = jnp.zeros_like(error)
     for k, piece in sent:
         error_out = lax.dynamic_update_slice(

time: 626 us -> 622 us (level)
  waiting for transfers between devices: 305 us -> 298 us
    ppermute x3, waiting for transfers between devices: 68.8 us -> 59.9 us  [step_on_device(): piece = lax.ppermute(piece, 'wide', [(i, i ^ k) for i in range(groups)])]
    pallas_call x2 -> x3, Pallas kernels: 29.5 us -> 34.1 us  [grad_rows(): pl.pallas_call(body, grid_spec=pltpu.PrefetchScalarGridSpec(num_scalar_pr...]
  transfers between devices with their start and end apart: 54 -> 54, of which waited for: 20 -> 20; matrix products, arithmetic and copies ran while one was open for 18% -> 18% of each run, Pallas kernels for 17% -> 18%
where the time goes in v3:
time: 622 us; the launch traced here: 619 us
  waiting for transfers between devices  298 us (48%)
  Pallas kernels  117 us (19%)
  local copies, waits for them, and re-layouts  96 us (15%)
  starting transfers between devices  52.2 us (8%)
  between operations  36.1 us (6%)
  other arithmetic  11.7 us (2%)
  matrix products  8.22 us (1%)
    ppermute x28, waiting for transfers between devices, ring_gather(): got = lax.ppermute(moving[way, part], axis, back if way else ahead)  108 us
    ppermute x3, waiting for transfers between devices, step_on_device(): piece = lax.ppermute(piece, 'wide', [(i, i ^ k) for i in range(groups)])  59.9 us
    ppermute x9, waiting for transfers between devices, wide_pieces(): lax.ppermute(pieces[k & k - 1], axis, [(i, i ^ bit) for i in range(count)])  48.1 us
    all_gather x3, waiting for transfers between devices, listed_gather(): lax.all_gather(shard, axis, axis=1, tiled=True, axis_index_groups=[order])  46.2 us
    pallas_call x4, Pallas kernels, predict(): pl.pallas_call(body, grid_spec=pltpu.PrefetchScalarGridSpec(num_scalar_pr...  43.8 us
    dynamic_update_slice x28, local copies, waits for them, and re-layouts, ring_gather(): full = lax.dynamic_update_slice(full, got, (part * half, source * width))  36.1 us
    ppermute x4, waiting for transfers between devices, head_pieces(): got.append(lax.ppermute(part, axis, perm))  34.2 us
    pallas_call x3, Pallas kernels, grad_rows(): pl.pallas_call(body, grid_spec=pltpu.PrefetchScalarGridSpec(num_scalar_pr...  34.1 us
  transfers between devices with their start and end apart: 54, of which 20 were waited for; matrix products, arithmetic and copies ran while one was open for 18% of the time, Pallas kernels for 18%

profile of v3, /device:TPU:0, one launch (start us, length us, event | category | flops | bytes accessed | tf_op | source)
XLA Modules:
  0.0 619.1 jit_solution(7153355858163235598)
XLA Ops:
  8.7 4.9 convert_element_type.25
  13.6 3.0 collective-permute-start.8
  19.2 5.8 all-to-all-start
  25.8 5.7 collective-permute-start.1
  32.6 33.1 %collective-permute-done.1 = bf16[1024,64]{0,1:T(8,128)(2,1)S(1)} collective-permute-done((bf16[1024,64]{0,1:T(8,128)(2,1)S(1)}, bf16[1024,64]{0,1:T(8,128)(2,1)S(1)}, u32[]{:S(2)}, u32[]{:S(2)}) %collective-permute-start.1) | collective-permute-done | bytes 131104 | tf_op jit(solution)/shard_map/ppermute | solution.py:95
  65.7 19.3 %collective-permute-done.8 = bf16[3072,512]{1,0:T(8,128)(2,1)} collective-permute-done((bf16[3072,512]{1,0:T(8,128)(2,1)}, bf16[3072,512]{1,0:T(8,128)(2,1)}, u32[]{:S(2)}, u32[]{:S(2)}) %collective-permute-start.8) | collective-permute-done | bytes 3145760 | tf_op jit(solution)/shard_map/ppermute | solution.py:75
  95.2 18.7 %collective-permute-done.11 = bf16[1024,512]{1,0:T(8,128)(2,1)} collective-permute-done((bf16[1024,512]{1,0:T(8,128)(2,1)S(1)}, bf16[1024,512]{1,0:T(8,128)(2,1)}, u32[]{:S(2)}, u32[]{:S(2)}) %collective-permute-start.11) | collective-permute-done | bytes 1048608 | tf_op jit(solution)/shard_map/ppermute | solution.py:75
  113.9 9.6 %collective-permute-done.5 = bf16[1024,256]{1,0:T(8,128)(2,1)} collective-permute-done((bf16[1024,256]{1,0:T(8,128)(2,1)S(1)}, bf16[1024,256]{1,0:T(8,128)(2,1)}, u32[]{:S(2)}, u32[]{:S(2)}) %collective-permute-start.5) | collective-permute-done | bytes 524320 | tf_op jit(solution)/shard_map/ppermute | solution.py:75
  144.9 13.8 %project.1 = (bf16[1024,512]{1,0:T(8,128)(2,1)}, bf16[1024,128]{1,0:T(8,128)(2,1)}, bf16[1024,128]{1,0:T(8,128)(2,1)}) custom-call(bf16[1024,4096]{1,0:T(8,128)(2,1)} %all-gather.4.cloned.1.call-done.hidden_ref, f32[1,4096]{1,0:T(1,128)} %bitcast.88, bf16[4096,512]{1,0:T(8,128)(2,1)} %query_ref.1, bf16[4096,256]{1,0:T(8,128)(2,1)} %copy-done.5, ...), custom_call_target="tpu_custom_call" | custom-call | flops 6442450944 | bytes 8388608 | tf_op jit(solution)/shard_map/project/pallas_call | solution.py:138
  158.7 9.3 %attend.1 = bf16[1024,512]{1,0:T(8,128)(2,1)} custom-call(bf16[1024,512]{1,0:T(8,128)(2,1)} %get-tuple-element.37.q_ref, bf16[1024,128]{1,0:T(8,128)(2,1)} %get-tuple-element.38.k0_ref.k1_ref, bf16[1024,128]{1,0:T(8,128)(2,1)} %get-tuple-element.38.k0_ref.k1_ref, bf16[1024,128]{1,0:T(8,128)(2,1)} %get-tuple-element.39.v0_ref.v1_ref, ...), custom_call_target="tpu_custom_call" | custom-call | flops 4294967296 | bytes 2097152 | tf_op jit(solution)/shard_map/attend/pallas_call | solution.py:208
  173.3 2.3 constant_dynamic-update-slice_fusion.24
  175.7 2.5 broadcast_in_dim.34
  179.2 2.3 constant_dynamic-update-slice_fusion.11
  181.5 2.3 constant_dynamic-update-slice_fusion.10
  183.7 5.2 broadcast_in_dim.33
  189.0 3.7 constant_dynamic-update-slice_fusion.19
  192.7 3.8 constant_dynamic-update-slice_fusion.18
  196.5 3.9 constant_dynamic-update-slice_fusion.17
  200.4 2.3 constant_dynamic-update-slice_fusion.9
  202.6 3.9 constant_dynamic-update-slice_fusion.16.refs_1_
  208.6 9.2 %collective-permute-done.15 = bf16[512,512]{1,0:T(8,128)(2,1)S(1)} collective-permute-done((bf16[512,512]{1,0:T(8,128)(2,1)S(1)}, bf16[512,512]{1,0:T(8,128)(2,1)S(1)}, u32[]{:S(2)}, u32[]{:S(2)}) %collective-permute-start.15) | collective-permute-done | bytes 524320 | tf_op jit(solution)/shard_map/ppermute | solution.py:52
  219.8 46.2 %all-gather.6.cloned.1.call-done.refs_0_ = bf16[1024,4096]{1,0:T(8,128)(2,1)} async-done(((bf16[1024,512]{1,0:T(8,128)(2,1)}), bf16[1024,4096]{1,0:T(8,128)(2,1)}) %all-gather.6.cloned.1.call-update) | async-done | bytes 8388624 | tf_op jit(solution)/shard_map/all_gather | solution.py:67
  266.5 12.3 %predict.4.refs_2_ = f32[1024,512]{1,0:T(8,128)} custom-call(s32[8]{0:T(128)} %iota.19.places_ref, s32[8]{0:T(128)} %constant.215.clone.table_ref, bf16[1024,4096]{1,0:T(8,128)(2,1)} %all-gather.6.cloned.1.call-done.refs_0_, bf16[12288,512]{1,0:T(8,128)(2,1)} %constant_dynamic-update-slice_fusion.16.refs_1_), custom_call_target="tpu_custom_call" | custom-call | flops 4294967296 | bytes 8388608 | tf_op jit(solution)/shard_map/predict/pallas_call | solution.py:286
  287.4 1.9 constant_dynamic-update-slice_fusion.20
  289.3 1.9 constant_dynamic-update-slice_fusion.40
  291.2 15.4 %collective-permute-done.21 = bf16[512,512]{1,0:T(8,128)(2,1)S(1)} collective-permute-done((bf16[512,512]{1,0:T(8,128)(2,1)S(1)}, bf16[512,512]{1,0:T(8,128)(2,1)S(1)}, u32[]{:S(2)}, u32[]{:S(2)}) %collective-permute-start.21) | collective-permute-done | bytes 524320 | tf_op jit(solution)/shard_map/ppermute | solution.py:52
  308.2 20.5 %collective-permute-done.23 = bf16[512,512]{1,0:T(8,128)(2,1)S(1)} collective-permute-done((bf16[512,512]{1,0:T(8,128)(2,1)}, bf16[512,512]{1,0:T(8,128)(2,1)S(1)}, u32[]{:S(2)}, u32[]{:S(2)}) %collective-permute-start.23) | collective-permute-done | bytes 524320 | tf_op jit(solution)/shard_map/ppermute | solution.py:52
  336.6 18.9 %collective-permute-done.25 = bf16[512,512]{1,0:T(8,128)(2,1)S(1)} collective-permute-done((bf16[512,512]{1,0:T(8,128)(2,1)S(1)}, bf16[512,512]{1,0:T(8,128)(2,1)S(1)}, u32[]{:S(2)}, u32[]{:S(2)}) %collective-permute-start.25) | collective-permute-done | bytes 524320 | tf_op jit(solution)/shard_map/ppermute | solution.py:52
  358.6 8.2 %convert_add_fusion = f32[1024,512]{1,0:T(8,128)S(1)} fusion(bf16[1024,512]{1,0:T(8,128)(2,1)S(1)} %copy-done.7, bf16[1024,4096]{1,0:T(8,128)(2,1)} %constant_dynamic-update-slice_fusion.36, bf16[4096,512]{1,0:T(8,128)(2,1)} %bitcast.40), kind=kOutput, calls=%fused_computation.2 | convolution fusion | flops 4296015872 | bytes 15728640 | tf_op jit(solution)/shard_map/dot_general | solution.py:471
  380.1 15.3 %collective-permute-done.27 = bf16[512,512]{1,0:T(8,128)(2,1)} collective-permute-done((bf16[512,512]{1,0:T(8,128)(2,1)}, bf16[512,512]{1,0:T(8,128)(2,1)}, u32[]{:S(2)}, u32[]{:S(2)}) %collective-permute-start.27) | collective-permute-done | bytes 524320 | tf_op jit(solution)/shard_map/ppermute | solution.py:52
  397.5 13.9 %collective-permute-done.29 = bf16[512,512]{1,0:T(8,128)(2,1)} collective-permute-done((bf16[512,512]{1,0:T(8,128)(2,1)}, bf16[512,512]{1,0:T(8,128)(2,1)}, u32[]{:S(2)}, u32[]{:S(2)}) %collective-permute-start.29) | collective-permute-done | bytes 524320 | tf_op jit(solution)/shard_map/ppermute | solution.py:52
  413.9 13.1 %predict.5.refs_2_ = f32[1024,512]{1,0:T(8,128)} custom-call(s32[8]{0:T(128)} %iota.20.places_ref, s32[8]{0:T(128)} %constant.215.clone.table_ref, bf16[1024,4096]{1,0:T(8,128)(2,1)} %all-gather.8.cloned.1.call-done.refs_0_.refs_1_, bf16[12288,512]{1,0:T(8,128)(2,1)} %constant_dynamic-update-slice_fusion.16.refs_1_, f32[1024,512]{1,0:T(8,128)} %predict.4.refs_2_), custom_call_target="tpu_custom_call" | custom-call | flops 4294967296 | bytes 8388608 | tf_op jit(solution)/shard_map/predict/pallas_call | solution.py:286
  428.9 1.9 constant_dynamic-update-slice_fusion.6
  430.9 1.9 constant_dynamic-update-slice_fusion.35
  437.8 1.9 constant_dynamic-update-slice_fusion.5
  439.7 1.9 constant_dynamic-update-slice_fusion.4
  441.6 1.9 constant_dynamic-update-slice_fusion.33
  445.5 2.5 collective-permute-done.35
  448.2 7.8 %collective-permute-done.37 = bf16[512,512]{1,0:T(8,128)(2,1)S(1)} collective-permute-done((bf16[512,512]{1,0:T(8,128)(2,1)}, bf16[512,512]{1,0:T(8,128)(2,1)S(1)}, u32[]{:S(2)}, u32[]{:S(2)}) %collective-permute-start.37) | collective-permute-done | bytes 524320 | tf_op jit(solution)/shard_map/ppermute | solution.py:52
  461.7 1.9 constant_dynamic-update-slice_fusion.30.refs_0_
  463.6 12.1 %predict.6.refs_2_ = f32[1024,512]{1,0:T(8,128)} custom-call(s32[7]{0:T(128)} %pad_add_fusion.places_ref.table_ref, s32[7]{0:T(128)} %pad_add_fusion.places_ref.table_ref, bf16[1024,4096]{1,0:T(8,128)(2,1)} %constant_dynamic-update-slice_fusion.30.refs_0_, bf16[12288,512]{1,0:T(8,128)(2,1)} %constant_dynamic-update-slice_fusion.16.refs_1_, ...), custom_call_target="tpu_custom_call" | custom-call | flops 3758096384 | bytes 7340032 | tf_op jit(solution)/shard_map/predict/pallas_call | solution.py:286
  480.7 6.3 %predict.7 = (f32[1024,512]{1,0:T(8,128)}, bf16[1024,512]{1,0:T(8,128)(2,1)}) custom-call(s32[1]{0:T(128)} %slice.36.places_ref.table_ref, s32[1]{0:T(128)} %slice.36.places_ref.table_ref, bf16[1024,4096]{1,0:T(8,128)(2,1)} %constant_dynamic-update-slice_fusion.29.refs_0_.refs_2_, bf16[12288,512]{1,0:T(8,128)(2,1)} %constant_dynamic-update-slice_fusion.16.refs_1_, ...), custom_call_target="tpu_custom_call" | custom-call | flops 536870912 | bytes 1048576 | tf_op jit(solution)/shard_map/predict/pallas_call | solution.py:286
  493.8 9.7 %grad_rows.5 = bf16[1536,512]{1,0:T(8,128)(2,1)} custom-call(s32[1]{0:T(128)} %bitcast.57.first_ref, s32[24]{0:T(128)} %constant.219.table_ref, bf16[1024,4096]{1,0:T(8,128)(2,1)} %all-gather.6.cloned.1.call-done.refs_0_, bf16[1024,4096]{1,0:T(8,128)(2,1)} %all-gather.8.cloned.1.call-done.refs_0_.refs_1_, ...), custom_call_target="tpu_custom_call" | custom-call | flops 3221225472 | bytes 6291456 | tf_op jit(solution)/shard_map/grad_rows/pallas_call | solution.py:345
  504.5 9.4 %grad_rows.4 = bf16[1536,512]{1,0:T(8,128)(2,1)} custom-call(s32[1]{0:T(128)} %bitcast.56.first_ref, s32[24]{0:T(128)} %constant.219.table_ref, bf16[1024,4096]{1,0:T(8,128)(2,1)} %all-gather.6.cloned.1.call-done.refs_0_, bf16[1024,4096]{1,0:T(8,128)(2,1)} %all-gather.8.cloned.1.call-done.refs_0_.refs_1_, ...), custom_call_target="tpu_custom_call" | custom-call | flops 3221225472 | bytes 6291456 | tf_op jit(solution)/shard_map/grad_rows/pallas_call | solution.py:345
  519.7 59.9 %collective-permute-done.42 = bf16[256,512]{1,0:T(8,128)(2,1)} collective-permute-done((bf16[256,512]{1,0:T(8,128)(2,1)S(1)}, bf16[256,512]{1,0:T(8,128)(2,1)}, u32[]{:S(2)}, u32[]{:S(2)}) %collective-permute-start.42) | collective-permute-done | bytes 262176 | tf_op jit(solution)/shard_map/ppermute | solution.py:500
  581.7 15.0 %grad_rows.3.grads_ref = f32[3072,512]{1,0:T(8,128)} custom-call(s32[1]{0:T(128)} %bitcast.55.first_ref, s32[24]{0:T(128)} %constant.219.table_ref, bf16[1024,4096]{1,0:T(8,128)(2,1)} %all-gather.6.cloned.1.call-done.refs_0_, bf16[1024,4096]{1,0:T(8,128)(2,1)} %all-gather.8.cloned.1.call-done.refs_0_.refs_1_, ...), custom_call_target="tpu_custom_call" | custom-call | flops 6442450944 | bytes 12582912 | tf_op jit(solution)/shard_map/grad_rows/pallas_call | solution.py:345
  596.7 7.9 %update.2 = (f32[3072,512]{1,0:T(8,128)}, f32[3072,512]{1,0:T(8,128)}) custom-call(f32[3072,512]{1,0:T(8,128)} %grad_rows.3.grads_ref, f32[3072,512]{1,0:T(8,128)} %joining_ref.3, f32[3072,512]{1,0:T(8,128)} %momentum_ref.3, bf16[1536,512]{1,0:T(8,128)(2,1)} %collective-permute-done.49.refs_0_), custom_call_target="tpu_custom_call" | custom-call | flops 4718592 | bytes 17301504 | tf_op jit(solution)/shard_map/update/pallas_call | solution.py:379
  604.6 7.9 %update.3 = (f32[3072,512]{1,0:T(8,128)}, f32[3072,512]{1,0:T(8,128)}) custom-call(f32[3072,512]{1,0:T(8,128)} %grad_rows.3.grads_ref, f32[3072,512]{1,0:T(8,128)} %joining_ref.3, f32[3072,512]{1,0:T(8,128)} %momentum_ref.3, bf16[1536,512]{1,0:T(8,128)(2,1)} %collective-permute-done.48.refs_0_, ...), custom_call_target="tpu_custom_call", output_to_operand_aliasing={{0}: (4, {}), {1}: (5, {})} | custom-call | flops 4718592 | bytes 17301504 | tf_op jit(solution)/shard_map/update/pallas_call | solution.py:379
  (190 shorter events, 100.9 us)
Async XLA Ops:
  7.2 136.4 %all-gather.4.cloned.1.call-start = ((), (), s32[]{:S(2)}) async-start(), calls=%async_computation.1 | async-start | bytes 9437184 | tf_op jit(solution)/shard_map/all_gather | solution.py:67
  7.9 258.0 %all-gather.6.cloned.1.call-start = ((), (), s32[]{:S(2)}) async-start(), calls=%async_computation.2 | async-start | bytes 9437184 | tf_op jit(solution)/shard_map/all_gather | solution.py:67
  8.7 404.7 %all-gather.8.cloned.1.call-start = ((), (), s32[]{:S(2)}) async-start(), calls=%async_computation.3 | async-start | bytes 9437184 | tf_op jit(solution)/shard_map/all_gather | solution.py:67
  13.6 71.4 %collective-permute-start.8 = (bf16[3072,512]{1,0:T(8,128)(2,1)}, bf16[3072,512]{1,0:T(8,128)(2,1)}, u32[]{:S(2)}, u32[]{:S(2)}) collective-permute-start(bf16[3072,512]{1,0:T(8,128)(2,1)} %convert_element_type.25), channel_id=1, source_target_pairs={{0,16},{8,24},{16,0},{24,8},{1,17},{9,25},{17,1},{25,9},{2,18},{10... | collective-permute-start | bytes 9437192 | tf_op jit(solution)/shard_map/ppermute | solution.py:75
  19.2 67.0 %all-to-all-start = ((bf16[128,8,512]{0,2,1:T(8,128)(2,1)}), bf16[128,8,512]{0,2,1:T(8,128)(2,1)S(1)}, u32[]{:S(2)}, u32[]{:S(2)}) async-start(bf16[128,8,512]{0,2,1:T(8,128)(2,1)} %bitcast.10), calls=%async_computation | async-start | bytes 2097152 | tf_op jit(solution)/shard_map/all_to_all | solution.py:425
  25.8 39.9 %collective-permute-start.1 = (bf16[1024,64]{0,1:T(8,128)(2,1)S(1)}, bf16[1024,64]{0,1:T(8,128)(2,1)S(1)}, u32[]{:S(2)}, u32[]{:S(2)}) collective-permute-start(bf16[1024,64]{0,1:T(8,128)(2,1)S(1)} %constant_dynamic-slice_fusion.5), channel_id=1, source_target_pairs={{1,0},{4,1},{5,2},{0,3},{3,4},{6,5},{7,6},{2,7},{9,8},{12,9},{13,1... | collective-permute-start | bytes 393224 | tf_op jit(solution)/shard_map/ppermute | solution.py:95
  31.4 53.5 %collective-permute-start.2 = (bf16[1024,64]{0,1:T(8,128)(2,1)S(1)}, bf16[1024,64]{0,1:T(8,128)(2,1)S(1)}, u32[]{:S(2)}, u32[]{:S(2)}) collective-permute-start(bf16[1024,64]{0,1:T(8,128)(2,1)S(1)} %constant_dynamic-slice_fusion.5), channel_id=1, source_target_pairs={{4,0},{5,1},{0,2},{1,3},{6,4},{7,5},{2,6},{3,7},{12,8},{13,9},{8,1... | collective-permute-start | bytes 393224 | tf_op jit(solution)/shard_map/ppermute | solution.py:95
  31.4 54.7 %collective-permute-start.3 = (bf16[1024,64]{0,1:T(8,128)(2,1)S(1)}, bf16[1024,64]{0,1:T(8,128)(2,1)S(1)}, u32[]{:S(2)}, u32[]{:S(2)}) collective-permute-start(bf16[1024,64]{0,1:T(8,128)(2,1)S(1)} %constant_dynamic-slice_fusion.5), channel_id=1, source_target_pairs={{5,0},{0,1},{1,2},{4,3},{7,4},{2,5},{3,6},{6,7},{13,8},{8,9},{9,10... | collective-permute-start | bytes 393224 | tf_op jit(solution)/shard_map/ppermute | solution.py:95
  32.5 111.0 %collective-permute-start.7 = (bf16[3072,512]{1,0:T(8,128)(2,1)}, bf16[3072,512]{1,0:T(8,128)(2,1)}, u32[]{:S(2)}, u32[]{:S(2)}) collective-permute-start(bf16[3072,512]{1,0:T(8,128)(2,1)} %convert_element_type.25), channel_id=1, source_target_pairs={{0,8},{8,0},{16,24},{24,16},{1,9},{9,1},{17,25},{25,17},{2,10},{10... | collective-permute-start | bytes 9437192 | tf_op jit(solution)/shard_map/ppermute | solution.py:75
  84.9 58.6 %collective-permute-start.9 = (bf16[3072,512]{1,0:T(8,128)(2,1)}, bf16[3072,512]{1,0:T(8,128)(2,1)}, u32[]{:S(2)}, u32[]{:S(2)}) collective-permute-start(bf16[3072,512]{1,0:T(8,128)(2,1)} %collective-permute-done.8), channel_id=1, source_target_pairs={{0,8},{8,0},{16,24},{24,16},{1,9},{9,1},{17,25},{25,17},{2,10},{10... | collective-permute-start | bytes 9437192 | tf_op jit(solution)/shard_map/ppermute | solution.py:75
  87.7 26.2 %collective-permute-start.11 = (bf16[1024,512]{1,0:T(8,128)(2,1)S(1)}, bf16[1024,512]{1,0:T(8,128)(2,1)}, u32[]{:S(2)}, u32[]{:S(2)}) collective-permute-start(bf16[1024,512]{1,0:T(8,128)(2,1)S(1)} %bitcast.77), channel_id=1, source_target_pairs={{0,16},{8,24},{16,0},{24,8},{1,17},{9,25},{17,1},{25,9},{2,18},{10... | collective-permute-start | bytes 3145736 | tf_op jit(solution)/shard_map/ppermute | solution.py:75
  93.3 30.3 %collective-permute-start.5 = (bf16[1024,256]{1,0:T(8,128)(2,1)S(1)}, bf16[1024,256]{1,0:T(8,128)(2,1)}, u32[]{:S(2)}, u32[]{:S(2)}) collective-permute-start(bf16[1024,256]{1,0:T(8,128)(2,1)S(1)} %get-tuple-element.77), channel_id=1, source_target_pairs={{0,16},{8,24},{16,0},{24,8},{1,17},{9,25},{17,1},{25,9},{2,18},{10... | collective-permute-start | bytes 1572872 | tf_op jit(solution)/shard_map/ppermute | solution.py:75
  94.9 48.6 %collective-permute-start.10 = (bf16[1024,512]{1,0:T(8,128)(2,1)S(1)}, bf16[1024,512]{1,0:T(8,128)(2,1)}, u32[]{:S(2)}, u32[]{:S(2)}) collective-permute-start(bf16[1024,512]{1,0:T(8,128)(2,1)S(1)} %bitcast.78), channel_id=1, source_target_pairs={{0,8},{8,0},{16,24},{24,16},{1,9},{9,1},{17,25},{25,17},{2,10},{10... | collective-permute-start | bytes 3145736 | tf_op jit(solution)/shard_map/ppermute | solution.py:75
  113.9 29.7 %collective-permute-start.12 = (bf16[1024,512]{1,0:T(8,128)(2,1)}, bf16[1024,512]{1,0:T(8,128)(2,1)}, u32[]{:S(2)}, u32[]{:S(2)}) collective-permute-start(bf16[1024,512]{1,0:T(8,128)(2,1)} %collective-permute-done.11), channel_id=1, source_target_pairs={{0,8},{8,0},{16,24},{24,16},{1,9},{9,1},{17,25},{25,17},{2,10},{10... | collective-permute-start | bytes 3145736 | tf_op jit(solution)/shard_map/ppermute | solution.py:75
  123.5 18.9 %collective-permute-start.6 = (bf16[1024,256]{1,0:T(8,128)(2,1)}, bf16[1024,256]{1,0:T(8,128)(2,1)}, u32[]{:S(2)}, u32[]{:S(2)}) collective-permute-start(bf16[1024,256]{1,0:T(8,128)(2,1)} %collective-permute-done.5), channel_id=1, source_target_pairs={{0,8},{8,0},{16,24},{24,16},{1,9},{9,1},{17,25},{25,17},{2,10},{10... | collective-permute-start | bytes 1572872 | tf_op jit(solution)/shard_map/ppermute | solution.py:75
  169.2 37.3 %collective-permute-start.13 = (bf16[512,512]{1,0:T(8,128)(2,1)S(1)}, bf16[512,512]{1,0:T(8,128)(2,1)S(1)}, u32[]{:S(2)}, u32[]{:S(2)}) collective-permute-start(bf16[512,512]{1,0:T(8,128)(2,1)S(1)} %get-tuple-element.74), channel_id=1, source_target_pairs={{0,2},{2,4},{4,6},{6,7},{7,5},{5,3},{3,1},{1,0},{8,10},{10,12},{12... | collective-permute-start | bytes 1572872 | tf_op jit(solution)/shard_map/ppermute | solution.py:52
  171.1 37.3 %collective-permute-start.14 = (bf16[512,512]{1,0:T(8,128)(2,1)S(1)}, bf16[512,512]{1,0:T(8,128)(2,1)S(1)}, u32[]{:S(2)}, u32[]{:S(2)}) collective-permute-start(bf16[512,512]{1,0:T(8,128)(2,1)S(1)} %get-tuple-element.74), channel_id=1, source_target_pairs={{2,0},{4,2},{6,4},{7,6},{5,7},{3,5},{1,3},{0,1},{10,8},{12,10},{14... | collective-permute-start | bytes 1572872 | tf_op jit(solution)/shard_map/ppermute | solution.py:52
  171.3 46.5 %collective-permute-start.15 = (bf16[512,512]{1,0:T(8,128)(2,1)S(1)}, bf16[512,512]{1,0:T(8,128)(2,1)S(1)}, u32[]{:S(2)}, u32[]{:S(2)}) collective-permute-start(bf16[512,512]{1,0:T(8,128)(2,1)S(1)} %get-tuple-element.73), channel_id=1, source_target_pairs={{0,2},{2,4},{4,6},{6,7},{7,5},{5,3},{3,1},{1,0},{8,10},{10,12},{12... | collective-permute-start | bytes 1572872 | tf_op jit(solution)/shard_map/ppermute | solution.py:52
  173.1 46.5 %collective-permute-start.16 = (bf16[512,512]{1,0:T(8,128)(2,1)S(1)}, bf16[512,512]{1,0:T(8,128)(2,1)S(1)}, u32[]{:S(2)}, u32[]{:S(2)}) collective-permute-start(bf16[512,512]{1,0:T(8,128)(2,1)S(1)} %get-tuple-element.73), channel_id=1, source_target_pairs={{2,0},{4,2},{6,4},{7,6},{5,7},{3,5},{1,3},{0,1},{10,8},{12,10},{14... | collective-permute-start | bytes 1572872 | tf_op jit(solution)/shard_map/ppermute | solution.py:52
  206.5 74.0 %collective-permute-start.17 = (bf16[512,512]{1,0:T(8,128)(2,1)S(1)}, bf16[512,512]{1,0:T(8,128)(2,1)S(1)}, u32[]{:S(2)}, u32[]{:S(2)}) collective-permute-start(bf16[512,512]{1,0:T(8,128)(2,1)S(1)} %collective-permute-done.13), channel_id=1, source_target_pairs={{0,2},{2,4},{4,6},{6,7},{7,5},{5,3},{3,1},{1,0},{8,10},{10,12},{12... | collective-permute-start | bytes 1572872 | tf_op jit(solution)/shard_map/ppermute | solution.py:52
  208.4 73.6 %collective-permute-start.18 = (bf16[512,512]{1,0:T(8,128)(2,1)S(1)}, bf16[512,512]{1,0:T(8,128)(2,1)}, u32[]{:S(2)}, u32[]{:S(2)}) collective-permute-start(bf16[512,512]{1,0:T(8,128)(2,1)S(1)} %collective-permute-done.14), channel_id=1, source_target_pairs={{2,0},{4,2},{6,4},{7,6},{5,7},{3,5},{1,3},{0,1},{10,8},{12,10},{14... | collective-permute-start | bytes 1572872 | tf_op jit(solution)/shard_map/ppermute | solution.py:52
  217.8 64.8 %collective-permute-start.19 = (bf16[512,512]{1,0:T(8,128)(2,1)S(1)}, bf16[512,512]{1,0:T(8,128)(2,1)}, u32[]{:S(2)}, u32[]{:S(2)}) collective-permute-start(bf16[512,512]{1,0:T(8,128)(2,1)S(1)} %collective-permute-done.15), channel_id=1, source_target_pairs={{0,2},{2,4},{4,6},{6,7},{7,5},{5,3},{3,1},{1,0},{8,10},{10,12},{12... | collective-permute-start | bytes 1572872 | tf_op jit(solution)/shard_map/ppermute | solution.py:52
  219.6 64.4 %collective-permute-start.20 = (bf16[512,512]{1,0:T(8,128)(2,1)S(1)}, bf16[512,512]{1,0:T(8,128)(2,1)S(1)}, u32[]{:S(2)}, u32[]{:S(2)}) collective-permute-start(bf16[512,512]{1,0:T(8,128)(2,1)S(1)} %collective-permute-done.16), channel_id=1, source_target_pairs={{2,0},{4,2},{6,4},{7,6},{5,7},{3,5},{1,3},{0,1},{10,8},{12,10},{14... | collective-permute-start | bytes 1572872 | tf_op jit(solution)/shard_map/ppermute | solution.py:52
  280.6 26.0 %collective-permute-start.21 = (bf16[512,512]{1,0:T(8,128)(2,1)S(1)}, bf16[512,512]{1,0:T(8,128)(2,1)S(1)}, u32[]{:S(2)}, u32[]{:S(2)}) collective-permute-start(bf16[512,512]{1,0:T(8,128)(2,1)S(1)} %collective-permute-done.17), channel_id=1, source_target_pairs={{0,2},{2,4},{4,6},{6,7},{7,5},{5,3},{3,1},{1,0},{8,10},{10,12},{12... | collective-permute-start | bytes 1572872 | tf_op jit(solution)/shard_map/ppermute | solution.py:52
  282.0 26.2 %collective-permute-start.22 = (bf16[512,512]{1,0:T(8,128)(2,1)}, bf16[512,512]{1,0:T(8,128)(2,1)S(1)}, u32[]{:S(2)}, u32[]{:S(2)}) collective-permute-start(bf16[512,512]{1,0:T(8,128)(2,1)} %collective-permute-done.18), channel_id=1, source_target_pairs={{2,0},{4,2},{6,4},{7,6},{5,7},{3,5},{1,3},{0,1},{10,8},{12,10},{14... | collective-permute-start | bytes 1572872 | tf_op jit(solution)/shard_map/ppermute | solution.py:52
  282.6 46.0 %collective-permute-start.23 = (bf16[512,512]{1,0:T(8,128)(2,1)}, bf16[512,512]{1,0:T(8,128)(2,1)S(1)}, u32[]{:S(2)}, u32[]{:S(2)}) collective-permute-start(bf16[512,512]{1,0:T(8,128)(2,1)} %collective-permute-done.19), channel_id=1, source_target_pairs={{0,2},{2,4},{4,6},{6,7},{7,5},{5,3},{3,1},{1,0},{8,10},{10,12},{12... | collective-permute-start | bytes 1572872 | tf_op jit(solution)/shard_map/ppermute | solution.py:52
  284.0 46.2 %collective-permute-start.24 = (bf16[512,512]{1,0:T(8,128)(2,1)S(1)}, bf16[512,512]{1,0:T(8,128)(2,1)S(1)}, u32[]{:S(2)}, u32[]{:S(2)}) collective-permute-start(bf16[512,512]{1,0:T(8,128)(2,1)S(1)} %collective-permute-done.20), channel_id=1, source_target_pairs={{2,0},{4,2},{6,4},{7,6},{5,7},{3,5},{1,3},{0,1},{10,8},{12,10},{14... | collective-permute-start | bytes 1572872 | tf_op jit(solution)/shard_map/ppermute | solution.py:52
  330.2 25.3 %collective-permute-start.25 = (bf16[512,512]{1,0:T(8,128)(2,1)S(1)}, bf16[512,512]{1,0:T(8,128)(2,1)S(1)}, u32[]{:S(2)}, u32[]{:S(2)}) collective-permute-start(bf16[512,512]{1,0:T(8,128)(2,1)S(1)} %collective-permute-done.21), channel_id=1, source_target_pairs={{0,2},{2,4},{4,6},{6,7},{7,5},{5,3},{3,1},{1,0},{8,10},{10,12},{12... | collective-permute-start | bytes 1572872 | tf_op jit(solution)/shard_map/ppermute | solution.py:52
  332.5 25.2 %collective-permute-start.26 = (bf16[512,512]{1,0:T(8,128)(2,1)S(1)}, bf16[512,512]{1,0:T(8,128)(2,1)S(1)}, u32[]{:S(2)}, u32[]{:S(2)}) collective-permute-start(bf16[512,512]{1,0:T(8,128)(2,1)S(1)} %collective-permute-done.24), channel_id=1, source_target_pairs={{2,0},{4,2},{6,4},{7,6},{5,7},{3,5},{1,3},{0,1},{10,8},{12,10},{14... | collective-permute-start | bytes 1572872 | tf_op jit(solution)/shard_map/ppermute | solution.py:52
  369.1 26.3 %collective-permute-start.27 = (bf16[512,512]{1,0:T(8,128)(2,1)}, bf16[512,512]{1,0:T(8,128)(2,1)}, u32[]{:S(2)}, u32[]{:S(2)}) collective-permute-start(bf16[512,512]{1,0:T(8,128)(2,1)} %get-tuple-element.72), channel_id=1, source_target_pairs={{0,2},{2,4},{4,6},{6,7},{7,5},{5,3},{3,1},{1,0},{8,10},{10,12},{12... | collective-permute-start | bytes 1572872 | tf_op jit(solution)/shard_map/ppermute | solution.py:52
  370.7 26.3 %collective-permute-start.28 = (bf16[512,512]{1,0:T(8,128)(2,1)}, bf16[512,512]{1,0:T(8,128)(2,1)}, u32[]{:S(2)}, u32[]{:S(2)}) collective-permute-start(bf16[512,512]{1,0:T(8,128)(2,1)} %get-tuple-element.72), channel_id=1, source_target_pairs={{2,0},{4,2},{6,4},{7,6},{5,7},{3,5},{1,3},{0,1},{10,8},{12,10},{14... | collective-permute-start | bytes 1572872 | tf_op jit(solution)/shard_map/ppermute | solution.py:52
  371.1 40.3 %collective-permute-start.29 = (bf16[512,512]{1,0:T(8,128)(2,1)}, bf16[512,512]{1,0:T(8,128)(2,1)}, u32[]{:S(2)}, u32[]{:S(2)}) collective-permute-start(bf16[512,512]{1,0:T(8,128)(2,1)} %get-tuple-element.71), channel_id=1, source_target_pairs={{0,2},{2,4},{4,6},{6,7},{7,5},{5,3},{3,1},{1,0},{8,10},{10,12},{12... | collective-permute-start | bytes 1572872 | tf_op jit(solution)/shard_map/ppermute | solution.py:52
  372.7 39.0 %collective-permute-start.30 = (bf16[512,512]{1,0:T(8,128)(2,1)}, bf16[512,512]{1,0:T(8,128)(2,1)S(1)}, u32[]{:S(2)}, u32[]{:S(2)}) collective-permute-start(bf16[512,512]{1,0:T(8,128)(2,1)} %get-tuple-element.71), channel_id=1, source_target_pairs={{2,0},{4,2},{6,4},{7,6},{5,7},{3,5},{1,3},{0,1},{10,8},{12,10},{14... | collective-permute-start | bytes 1572872 | tf_op jit(solution)/shard_map/ppermute | solution.py:52
  380.1 112.6 %collective-permute-start.44 = (bf16[1024,4096]{1,0:T(8,128)(2,1)}, bf16[1024,4096]{1,0:T(8,128)(2,1)}, u32[]{:S(2)}, u32[]{:S(2)}) collective-permute-start(bf16[1024,4096]{1,0:T(8,128)(2,1)} %all-gather.6.cloned.1.call-done.refs_0_), channel_id=1, source_target_pairs={{0,8},{8,0},{16,24},{24,16},{1,9},{9,1},{17,25},{25,17},{2,10},{10... | collective-permute-start | bytes 25165832 | tf_op jit(solution)/shard_map/ppermute | solution.py:457
  395.4 37.4 %collective-permute-start.31 = (bf16[512,512]{1,0:T(8,128)(2,1)}, bf16[512,512]{1,0:T(8,128)(2,1)}, u32[]{:S(2)}, u32[]{:S(2)}) collective-permute-start(bf16[512,512]{1,0:T(8,128)(2,1)} %collective-permute-done.27), channel_id=1, source_target_pairs={{0,2},{2,4},{4,6},{6,7},{7,5},{5,3},{3,1},{1,0},{8,10},{10,12},{12... | collective-permute-start | bytes 1572872 | tf_op jit(solution)/shard_map/ppermute | solution.py:52
  397.0 36.1 %collective-permute-start.32 = (bf16[512,512]{1,0:T(8,128)(2,1)}, bf16[512,512]{1,0:T(8,128)(2,1)}, u32[]{:S(2)}, u32[]{:S(2)}) collective-permute-start(bf16[512,512]{1,0:T(8,128)(2,1)} %collective-permute-done.28), channel_id=1, source_target_pairs={{2,0},{4,2},{6,4},{7,6},{5,7},{3,5},{1,3},{0,1},{10,8},{12,10},{14... | collective-permute-start | bytes 1572872 | tf_op jit(solution)/shard_map/ppermute | solution.py:52
  411.4 23.4 %collective-permute-start.33 = (bf16[512,512]{1,0:T(8,128)(2,1)}, bf16[512,512]{1,0:T(8,128)(2,1)}, u32[]{:S(2)}, u32[]{:S(2)}) collective-permute-start(bf16[512,512]{1,0:T(8,128)(2,1)} %collective-permute-done.29), channel_id=1, source_target_pairs={{0,2},{2,4},{4,6},{6,7},{7,5},{5,3},{3,1},{1,0},{8,10},{10,12},{12... | collective-permute-start | bytes 1572872 | tf_op jit(solution)/shard_map/ppermute | solution.py:52
  411.7 23.5 %collective-permute-start.34 = (bf16[512,512]{1,0:T(8,128)(2,1)S(1)}, bf16[512,512]{1,0:T(8,128)(2,1)}, u32[]{:S(2)}, u32[]{:S(2)}) collective-permute-start(bf16[512,512]{1,0:T(8,128)(2,1)S(1)} %collective-permute-done.30), channel_id=1, source_target_pairs={{2,0},{4,2},{6,4},{7,6},{5,7},{3,5},{1,3},{0,1},{10,8},{12,10},{14... | collective-permute-start | bytes 1572872 | tf_op jit(solution)/shard_map/ppermute | solution.py:52
  434.8 21.2 %collective-permute-start.37 = (bf16[512,512]{1,0:T(8,128)(2,1)}, bf16[512,512]{1,0:T(8,128)(2,1)S(1)}, u32[]{:S(2)}, u32[]{:S(2)}) collective-permute-start(bf16[512,512]{1,0:T(8,128)(2,1)} %collective-permute-done.33), channel_id=1, source_target_pairs={{0,2},{2,4},{4,6},{6,7},{7,5},{5,3},{3,1},{1,0},{8,10},{10,12},{12... | collective-permute-start | bytes 1572872 | tf_op jit(solution)/shard_map/ppermute | solution.py:52
  435.2 20.8 %collective-permute-start.38 = (bf16[512,512]{1,0:T(8,128)(2,1)}, bf16[512,512]{1,0:T(8,128)(2,1)}, u32[]{:S(2)}, u32[]{:S(2)}) collective-permute-start(bf16[512,512]{1,0:T(8,128)(2,1)} %collective-permute-done.34), channel_id=1, source_target_pairs={{2,0},{4,2},{6,4},{7,6},{5,7},{3,5},{1,3},{0,1},{10,8},{12,10},{14... | collective-permute-start | bytes 1572872 | tf_op jit(solution)/shard_map/ppermute | solution.py:52
  447.9 44.8 %collective-permute-start.45 = (bf16[1024,4096]{1,0:T(8,128)(2,1)}, bf16[1024,4096]{1,0:T(8,128)(2,1)}, u32[]{:S(2)}, u32[]{:S(2)}) collective-permute-start(bf16[1024,4096]{1,0:T(8,128)(2,1)} %all-gather.8.cloned.1.call-done.refs_0_.refs_1_), channel_id=1, source_target_pairs={{0,8},{8,0},{16,24},{24,16},{1,9},{9,1},{17,25},{25,17},{2,10},{10... | collective-permute-start | bytes 25165832 | tf_op jit(solution)/shard_map/ppermute | solution.py:458
  456.0 19.7 %collective-permute-start.39 = (bf16[512,512]{1,0:T(8,128)(2,1)}, bf16[512,512]{1,0:T(8,128)(2,1)S(1)}, u32[]{:S(2)}, u32[]{:S(2)}) collective-permute-start(bf16[512,512]{1,0:T(8,128)(2,1)} %collective-permute-done.35), channel_id=1, source_target_pairs={{0,2},{2,4},{4,6},{6,7},{7,5},{5,3},{3,1},{1,0},{8,10},{10,12},{12... | collective-permute-start | bytes 1572872 | tf_op jit(solution)/shard_map/ppermute | solution.py:52
  457.6 18.1 %collective-permute-start.40 = (bf16[512,512]{1,0:T(8,128)(2,1)}, bf16[512,512]{1,0:T(8,128)(2,1)S(1)}, u32[]{:S(2)}, u32[]{:S(2)}) collective-permute-start(bf16[512,512]{1,0:T(8,128)(2,1)} %collective-permute-done.38), channel_id=1, source_target_pairs={{2,0},{4,2},{6,4},{7,6},{5,7},{3,5},{1,3},{0,1},{10,8},{12,10},{14... | collective-permute-start | bytes 1572872 | tf_op jit(solution)/shard_map/ppermute | solution.py:52
  491.6 26.8 %collective-permute-start.41 = (bf16[256,512]{1,0:T(8,128)(2,1)S(1)}, bf16[256,512]{1,0:T(8,128)(2,1)}, u32[]{:S(2)}, u32[]{:S(2)}) collective-permute-start(bf16[256,512]{1,0:T(8,128)(2,1)S(1)} %get-tuple-element.70), channel_id=1, source_target_pairs={{0,24},{8,16},{16,8},{24,0},{1,25},{9,17},{17,9},{25,1},{2,26},{10... | collective-permute-start | bytes 786440 | tf_op jit(solution)/shard_map/ppermute | solution.py:500
  503.5 93.3 %collective-permute-start.49 = (bf16[1536,512]{1,0:T(8,128)(2,1)}, bf16[1536,512]{1,0:T(8,128)(2,1)}, u32[]{:S(2)}, u32[]{:S(2)}) collective-permute-start(bf16[1536,512]{1,0:T(8,128)(2,1)} %grad_rows.5), channel_id=1, source_target_pairs={{0,16},{8,24},{16,0},{24,8},{1,17},{9,25},{17,1},{25,9},{2,18},{10... | collective-permute-start | bytes 4718600 | tf_op jit(solution)/shard_map/ppermute | solution.py:528
  513.9 90.7 %collective-permute-start.48 = (bf16[1536,512]{1,0:T(8,128)(2,1)}, bf16[1536,512]{1,0:T(8,128)(2,1)}, u32[]{:S(2)}, u32[]{:S(2)}) collective-permute-start(bf16[1536,512]{1,0:T(8,128)(2,1)} %grad_rows.4), channel_id=1, source_target_pairs={{0,16},{8,24},{16,0},{24,8},{1,17},{9,25},{17,1},{25,9},{2,18},{10... | collective-permute-start | bytes 4718600 | tf_op jit(solution)/shard_map/ppermute | solution.py:528
  516.9 63.7 %collective-permute-start.43 = (f32[256,512]{1,0:T(8,128)S(1)}, f32[256,512]{1,0:T(8,128)S(1)}, u32[]{:S(2)}, u32[]{:S(2)}) collective-permute-start(f32[256,512]{1,0:T(8,128)S(1)} %constant_dynamic-slice_fusion.1), channel_id=1, source_target_pairs={{0,8},{8,0},{16,24},{24,16},{1,9},{9,1},{17,25},{25,17},{2,10},{10... | collective-permute-start | bytes 1572872 | tf_op jit(solution)/shard_map/ppermute | solution.py:500
  516.9 62.6 %collective-permute-start.42 = (bf16[256,512]{1,0:T(8,128)(2,1)S(1)}, bf16[256,512]{1,0:T(8,128)(2,1)}, u32[]{:S(2)}, u32[]{:S(2)}) collective-permute-start(bf16[256,512]{1,0:T(8,128)(2,1)S(1)} %get-tuple-element.69), channel_id=1, source_target_pairs={{0,16},{8,24},{16,0},{24,8},{1,17},{9,25},{17,1},{25,9},{2,18},{10... | collective-permute-start | bytes 786440 | tf_op jit(solution)/shard_map/ppermute | solution.py:500
  (19 other events, 594.4 us)
Sparse Core Ops, SparseCore 0:
  9.5 117.5 all-gather.3
  128.7 137.2 all-gather.5
  267.5 138.1 all-gather.7
